TPU v7x, 256 devices: a whole 4x4x8 slice. The times are simulated.
256 devices in a mesh: line: 16 (over y, x), bus: 16 (over z, core).
Axes of the slice: x: 4, y: 4, z: 8, core: 2. Of those that a mesh axis runs over, the one named last changes fastest.
Arguments:
- primal: float32 [49152], P('line'), may hold values from 0.1 to 10
- slacks: float32 [49152], P('line'), may hold values from 0.1 to 10
- line_cost: float32 [49152], P('line'), may hold values from -6 to 6
- bus_dual: float32 [65536], P('bus'), may hold values from -6 to 6
- demand: float32 [65536], P('bus'), may hold values from -6 to 6
- endpoints: int32 [2, 49152], P(None, 'line'), may hold values from 0 to 65535, as said below
- fixed_part: float32 [256, 256, 256], P('bus'), as said below
Outputs:
- step_primal: float32 [49152], P('line')
- step_slack: float32 [49152], P('line')
- step_dual: float32 [65536], P('bus')
- step_lengths: float32 [2], replicated
Inputs may be any that keep to these rules, and one draw needn't show every extreme that they name: The two endpoints of every line differ. `fixed_part`: every block is symmetric and strictly diagonally dominant with a positive diagonal.
All inputs are finite; a program needn't handle non-finite values.
Results may differ from a plain program's by a relative error of at most 0.000043.
Values sent between devices are 32-bit elements; how exact they have to be, the bound alone decides.
A program may use at most 64 MiB of HBM per device.

v0:
```python
import jax
import jax.numpy as jnp
from jax import lax
from jax.sharding import Mesh
from jax.sharding import PartitionSpec as P

LINE = ("line_0", "line_1")


damping = 0.99


def from_everyone(x, axis):
    devices = lax.axis_size(axis)
    return lax.all_to_all(jnp.broadcast_to(x[None], (devices, *x.shape)), axis, 0, 0, tiled=True)


def taken_together(x, axis):
    everything = from_everyone(x, axis)
    return jnp.sum(everything, axis=0)


def in_blocks(x, dim, devices):
    shape = x.shape
    tiles = x.reshape(*shape[:dim], devices, shape[dim] // devices, *shape[dim + 1 :])
    return jnp.moveaxis(tiles, dim, 0)


def sum_together(arrays, axis, dims):
    devices = lax.axis_size(axis)
    tiles = [in_blocks(a, dim, devices) for a, dim in zip(arrays, dims)]
    lines = jnp.concatenate([b.reshape(devices, -1) for b in tiles], axis=1)
    rows = max(16, -(-lines.shape[1] // 1024) * 8)
    lines = jnp.pad(lines, ((0, 0), (0, rows * 128 - lines.shape[1]))).reshape(-1, 128)
    line, at, gathered = (lax.psum_scatter(lines, axis, tiled=True).reshape(-1), 0, [])
    for b in tiles:
        part = b[0]
        gathered.append(line[at : at + part.size].reshape(part.shape))
        at += part.size
    return tuple(gathered)


def over_axes(x, axes):
    for axis in axes:
        x = lax.psum(x, axis)
    return x


def laid_out(tiles, dim):
    shape = list(tiles.shape[1:])
    shape[dim] *= tiles.shape[0]
    return jnp.moveaxis(tiles, 0, dim).reshape(shape)


def collect(x, axis, dim):
    return laid_out(from_everyone(x, axis), dim)


def sent_and_summed(x, axis, dim):
    devices = lax.axis_size(axis)
    tiles = lax.all_to_all(in_blocks(x, dim, devices), axis, 0, 0, tiled=True)
    return jnp.sum(tiles, axis=0)


def over_axes_2(x, axes):
    for axis in axes:
        x = lax.pmin(x, axis)
    return x


def factor_solve(factor, right_side):
    lower_half = lax.linalg.triangular_solve(
        factor, right_side[..., None], left_side=True, lower=True
    )
    solved = lax.linalg.triangular_solve(
        factor, lower_half, left_side=True, lower=True, transpose_a=True
    )
    return solved[..., 0]


def per_device(primal, slacks, line_cost, bus_dual, demand, endpoints, fixed_part):
    lines_here = primal.shape[0]
    buses_here = bus_dual.shape[0]
    blocks_here = fixed_part.shape[0]
    block_size = fixed_part.shape[1]
    total_lines = lines_here * lax.axis_size(LINE)
    offset = lax.axis_index("bus") * buses_here
    local_from = endpoints[0] - offset
    local_to = endpoints[1] - offset
    slot_from = jnp.where((local_from >= 0) & (local_from < buses_here), local_from, buses_here)
    slot_to = jnp.where((local_to >= 0) & (local_to < buses_here), local_to, buses_here)
    own_from = slot_from
    own_to = slot_to

    def line_image(vector):
        padded = jnp.concatenate([vector, jnp.zeros((1,), jnp.float32)])
        partial_value = padded[own_from] - padded[own_to]
        return taken_together(partial_value, "bus")

    def bus_image(values, slot_from, slot_to):
        stacked = values.T
        spread = jax.ops.segment_sum(stacked, slot_from, buses_here + 1) - jax.ops.segment_sum(
            stacked, slot_to, buses_here + 1
        )
        return spread[:buses_here].T

    dual_res = line_cost - line_image(bus_dual) - slacks
    scaling = primal / slacks
    same_block = endpoints[0] // block_size == endpoints[1] // block_size
    crossing = jnp.where(same_block, -scaling, jnp.zeros_like(scaling))
    flat = jnp.zeros((buses_here * block_size,), jnp.float32)
    flat = flat.at[own_from * block_size + own_from % block_size].add(scaling, mode="drop")
    flat = flat.at[own_to * block_size + own_to % block_size].add(scaling, mode="drop")
    flat = flat.at[own_from * block_size + own_to % block_size].add(crossing, mode="drop")
    flat = flat.at[own_to * block_size + own_from % block_size].add(crossing, mode="drop")
    partial_blocks = flat.reshape(blocks_here, block_size, block_size)
    first_terms = bus_image(
        jnp.stack([primal, scaling * dual_res + primal, 1.0 / slacks]), own_from, own_to
    ).reshape(3, blocks_here, block_size)
    local_gap = jnp.sum(primal * slacks)
    owned = blocks_here // lax.axis_size(LINE)
    first_row = lax.axis_index(LINE) * owned
    normal, bus_terms = sum_together((partial_blocks, first_terms), LINE, (0, 1))
    gap_total = over_axes(local_gap, LINE)
    factor = jnp.linalg.cholesky(normal + lax.dynamic_slice_in_dim(fixed_part, first_row, owned, 0))
    owned_demand = lax.dynamic_slice_in_dim(
        demand.reshape(blocks_here, block_size), first_row, owned, 0
    )

    def solve_blocks(right_side):
        pieces = factor_solve(factor, right_side)
        return collect(pieces, LINE, 0).reshape(-1)

    residual_bus = owned_demand - bus_terms[0]
    gap_mean = gap_total / total_lines
    affine_dual = solve_blocks(residual_bus + bus_terms[1])
    affine_slack = dual_res - line_image(affine_dual)
    affine_primal = -primal - scaling * affine_slack
    ratio_primal = jnp.min(primal / jnp.maximum(-affine_primal, primal))
    ratio_slack = jnp.min(slacks / jnp.maximum(-affine_slack, slacks))
    step_aff_p, step_aff_d = (over_axes_2(ratio_primal, LINE), over_axes_2(ratio_slack, LINE))
    local_affine = jnp.sum(
        (primal + step_aff_p * affine_primal) * (slacks + step_aff_d * affine_slack)
    )
    gap_affine = over_axes(local_affine, LINE)
    centering = (gap_affine / gap_total) ** 3
    cross = affine_primal * affine_slack
    partial_value = bus_image((cross / slacks)[None], own_from, own_to)[0].reshape(
        blocks_here, block_size
    )
    extra = sent_and_summed(partial_value, LINE, 0)
    right_side = residual_bus + bus_terms[1] - centering * gap_mean * bus_terms[2] + extra
    step_dual = solve_blocks(right_side)
    step_slack = dual_res - line_image(step_dual)
    step_primal = (centering * gap_mean - primal * slacks - cross) / slacks - scaling * step_slack
    final_p, final_d = (
        over_axes_2(jnp.min(primal / jnp.maximum(-step_primal, primal)), LINE),
        over_axes_2(jnp.min(slacks / jnp.maximum(-step_slack, slacks)), LINE),
    )
    step_lengths = damping * jnp.stack([final_p, final_d])
    return (step_primal, step_slack, step_dual, step_lengths)


def solution(mesh):
    split = Mesh(mesh.devices.reshape(4, 4, mesh.shape["bus"]), ("line_0", "line_1", "bus"))
    in_specs = (P(LINE), P(LINE), P(LINE), P("bus"), P("bus"), P(None, LINE), P("bus", None, None))
    out_specs = (P(LINE), P(LINE), P("bus"), P())
    return jax.shard_map(
        per_device, mesh=split, in_specs=in_specs, out_specs=out_specs, check_vma=False
    )
```

profile of v0, /device:TPU:1, one launch (start us, length us, event | category | flops | bytes accessed | tf_op | source)
XLA Modules:
  0.0 620.3 jit_solution(12741704826375397293)
XLA Ops:
  7.2 0.9 compare_select_fusion
  9.0 17.4 %gather_fusion = f32[3072]{0:T(1024)S(1)} fusion(f32[4097]{0:T(1024)S(1)} %pad_maximum_fusion.2, s32[3072]{0:T(1024)S(1)} %broadcast_clamp_fusion.1), kind=kCustom, calls=%fused_computation | custom fusion | bytes 36864 | tf_op jit(solution)/shard_map/gather | solution.py:97
  26.4 17.4 %gather_fusion.1 = f32[3072]{0:T(1024)S(1)} fusion(f32[4097]{0:T(1024)S(1)} %pad_maximum_fusion.2, s32[3072]{0:T(1024)S(1)} %broadcast_clamp_fusion), kind=kCustom, calls=%fused_computation.1 | custom fusion | bytes 36864 | tf_op jit(solution)/shard_map/gather | solution.py:97
  44.6 10.0 %all-to-all-start = ((f32[16,1,3072]{2,1,0:T(1,128)}), f32[16,1,3072]{2,1,0:T(1,128)S(1)}, u32[]{:S(2)}, u32[]{:S(2)}) async-start(f32[16,1,3072]{2,1,0:T(1,128)} %broadcast_in_dim.29), calls=%async_computation | async-start | bytes 393216 | tf_op jit(solution)/shard_map/all_to_all | solution.py:15
  54.7 18.7 %scatter_custom_fusion = f32[1048576]{0:T(1024)} fusion(s32[3072]{0:T(1024)S(1)} %bitcast.252, f32[3072]{0:T(1024)S(1)} %get-tuple-element.71, f32[]{:T(128)} %constant.159.clone.1), kind=kCustom, calls=%fused_computation.19 | custom fusion | flops 3072 | bytes 4194308 | tf_op jit(solution)/shard_map/scatter-add | solution.py:112
  73.4 19.3 %scatter_fusion = f32[1048576]{0:T(1024)} fusion(f32[1048576]{0:T(1024)} %scatter_custom_fusion, s32[3072]{0:T(1024)S(1)} %bitcast.242, f32[3072]{0:T(1024)S(1)} %get-tuple-element.71), kind=kCustom, calls=%fused_computation.7 | custom fusion | flops 3072 | bytes 49152 | tf_op jit(solution)/shard_map/scatter-add | solution.py:113
  92.7 19.3 %scatter_fusion.1 = f32[1048576]{0:T(1024)} fusion(f32[1048576]{0:T(1024)} %scatter_fusion, s32[3072]{0:T(1024)S(1)} %bitcast.243, f32[3072]{0:T(1024)S(1)} %get-tuple-element.70), kind=kCustom, calls=%fused_computation.8 | custom fusion | flops 3072 | bytes 49152 | tf_op jit(solution)/shard_map/scatter-add | solution.py:114
  112.0 19.3 %scatter_fusion.2 = f32[1048576]{0:T(1024)} fusion(f32[1048576]{0:T(1024)} %scatter_fusion.1, s32[3072]{0:T(1024)S(1)} %bitcast.241, f32[3072]{0:T(1024)S(1)} %get-tuple-element.70), kind=kCustom, calls=%fused_computation.9 | custom fusion | flops 3072 | bytes 49152 | tf_op jit(solution)/shard_map/scatter-add | solution.py:115
  131.2 4.0 reshape_reshape_reshape.3
  135.4 1.7 copy.32
  137.0 21.1 %scatter_custom_fusion.5 = f32[4097,3]{1,0:T(8,128)S(1)} fusion(s32[3072]{0:T(1024)S(1)} %bitcast.238, f32[3072,3]{1,0:T(8,128)} %copy.32, f32[]{:T(128)} %constant.159.clone.1), kind=kCustom, calls=%fused_computation.39 | custom fusion | flops 9216 | bytes 49676 | tf_op jit(solution)/shard_map/scatter-add | solution.py:102
  158.2 22.1 %scatter_custom_fusion.4 = f32[4097,3]{1,0:T(8,128)} fusion(s32[3072]{0:T(1024)S(1)} %bitcast.247, f32[3072,3]{1,0:T(8,128)} %copy.32, f32[]{:T(128)} %constant.159.clone.1), kind=kCustom, calls=%fused_computation.41 | custom fusion | flops 9216 | bytes 49676 | tf_op jit(solution)/shard_map/scatter-add | solution.py:102
  180.3 3.1 slice_subtract_fusion
  183.4 2.2 copy.34
  185.6 4.4 select_maximum_fusion
  190.1 3.9 reshape.463
  194.0 1.0 constant_dynamic-slice_fusion.5
  196.4 113.0 %all-reduce.11.cloned.1.call-done = f32[8320,128]{1,0:T(8,128)} async-done(((f32[8320,128]{1,0:T(8,128)}), f32[8320,128]{1,0:T(8,128)}) %all-reduce.11.cloned.1.call-update) | async-done | bytes 4259856
  309.4 1.0 constant_dynamic-slice_fusion.3
  310.8 11.7 %custom-call.19 = f32[1,128,128]{2,1,0:T(8,128)S(1)} custom-call(f32[1,128,128]{2,1,0:T(8,128)S(1)} %cholesky.117), custom_call_target="Cholesky" | custom-call | tf_op jit(solution)/shard_map/jit(cholesky)/cholesky | solution.py:125
  322.6 9.8 %custom-call.20 = f32[1,1,128,128]{2,3,1,0:T(8,128)S(1)} custom-call(f32[1,1,128,128]{3,2,1,0:T(8,128)S(1)} %get-tuple-element.83), custom_call_target="InvertDiagBlocksLowerTriangular" | custom-call | tf_op jit(solution)/shard_map/jit(cholesky)/cholesky | solution.py:125
  332.9 11.7 %custom-call.21 = f32[1,128,128]{2,1,0:T(8,128)S(1)} custom-call(f32[1,128,128]{2,1,0:T(8,128)S(1)} %fusion.2), custom_call_target="Cholesky" | custom-call | tf_op jit(solution)/shard_map/jit(cholesky)/cholesky | solution.py:125
  346.7 4.0 while.8
  347.3 1.4 bitcast_dynamic-update-slice_fusion.3
  349.3 1.4 bitcast_dynamic-update-slice_fusion.3
  350.7 19.9 %custom-call.25 = f32[1,2,128,128]{2,3,1,0:T(8,128)S(1)} custom-call(f32[1,2,128,128]{3,2,1,0:T(8,128)S(1)} %bitcast.263), custom_call_target="InvertDiagBlocksLowerTriangular" | custom-call | tf_op jit(solution)/shard_map/triangular_solve/custom-call.4 | solution.py:75
  372.6 11.5 %all_to_all.33 = f32[16,1,256]{2,1,0:T(1,128)S(1)} all-to-all(f32[16,1,256]{2,1,0:T(1,128)S(1)} %broadcast_in_dim.34), channel_id=1, replica_groups=mesh['line_0'=4,'line_1'=4,'bus'=16] {'line_0','line_1'}, dimensions={0} | all-to-all | bytes 32768 | tf_op jit(solution)/shard_map/all_to_all | solution.py:15
  384.1 17.4 %gather_fusion.2 = f32[3072]{0:T(1024)S(1)} fusion(f32[4097]{0:T(1024)S(1)} %pad_maximum_fusion.1, s32[3072]{0:T(1024)S(1)} %broadcast_clamp_fusion.1), kind=kCustom, calls=%fused_computation.2 | custom fusion | bytes 36864 | tf_op jit(solution)/shard_map/gather | solution.py:97
  401.5 17.4 %gather_fusion.3 = f32[3072]{0:T(1024)S(1)} fusion(f32[4097]{0:T(1024)S(1)} %pad_maximum_fusion.1, s32[3072]{0:T(1024)S(1)} %broadcast_clamp_fusion), kind=kCustom, calls=%fused_computation.3 | custom fusion | bytes 36864 | tf_op jit(solution)/shard_map/gather | solution.py:97
  419.7 9.3 %all-to-all-start.2 = ((f32[16,1,3072]{2,1,0:T(1,128)}), f32[16,1,3072]{2,1,0:T(1,128)S(1)}, u32[]{:S(2)}, u32[]{:S(2)}) async-start(f32[16,1,3072]{2,1,0:T(1,128)} %broadcast_in_dim.35), calls=%async_computation.2 | async-start | bytes 393216 | tf_op jit(solution)/shard_map/all_to_all | solution.py:15
  429.0 10.2 %all-to-all-done.2 = f32[16,1,3072]{2,1,0:T(1,128)S(1)} async-done(((f32[16,1,3072]{2,1,0:T(1,128)}), f32[16,1,3072]{2,1,0:T(1,128)S(1)}, u32[]{:S(2)}, u32[]{:S(2)}) %all-to-all-start.2) | async-done | bytes 196640 | tf_op jit(solution)/shard_map/all_to_all | solution.py:15
  439.9 7.5 %all-reduce.8 = (f32[]{:T(128)}, f32[]{:T(128)}) all-reduce(f32[]{:T(128)} %get-tuple-element.39, f32[]{:T(128)} %get-tuple-element.38), channel_id=1, replica_groups=mesh['line_0'=4,'line_1'=4,'bus'=16] {'line_0'}, use_global_device_ids=true, to_apply=%region_17.20 | all-reduce | flops 2 | bytes 16 | tf_op jit(solution)/shard_map/pmin | solution.py:67
  447.4 7.5 %all-reduce.6 = (f32[]{:T(128)}, f32[]{:T(128)}) all-reduce(f32[]{:T(128)} %get-tuple-element.58, f32[]{:T(128)} %get-tuple-element.59), channel_id=1, replica_groups=mesh['line_0'=4,'line_1'=4,'bus'=16] {'line_1'}, use_global_device_ids=true, to_apply=%region_18.21 | all-reduce | flops 2 | bytes 16 | tf_op jit(solution)/shard_map/pmin | solution.py:67
  454.9 1.9 fusion.38
  456.8 20.3 %scatter_custom_fusion.7 = f32[4097]{0:T(1024)S(1)} fusion(s32[3072]{0:T(1024)S(1)} %bitcast.239, f32[3072]{0:T(1024)S(1)} %get-tuple-element.84, f32[]{:T(128)} %constant.159.clone.1), kind=kCustom, calls=%fused_computation.113 | custom fusion | flops 3072 | bytes 16392 | tf_op jit(solution)/shard_map/scatter-add | solution.py:102
  477.1 20.4 %scatter_custom_fusion.6 = f32[4097]{0:T(1024)S(1)} fusion(s32[3072]{0:T(1024)S(1)} %bitcast.248, f32[3072]{0:T(1024)S(1)} %get-tuple-element.84, f32[]{:T(128)} %constant.159.clone.1), kind=kCustom, calls=%fused_computation.115 | custom fusion | flops 3072 | bytes 16392 | tf_op jit(solution)/shard_map/scatter-add | solution.py:102
  497.5 7.7 %all-reduce.4 = (f32[]{:T(128)}, f32[]{:T(128)}) all-reduce(f32[]{:T(128)} %get-tuple-element.85, f32[]{:T(128)} %get-tuple-element.86), channel_id=1, replica_groups=mesh['line_0'=4,'line_1'=4,'bus'=16] {'line_0'}, use_global_device_ids=true, to_apply=%region_20.23 | all-reduce | flops 2 | bytes 16 | tf_op jit(solution)/shard_map/psum | solution.py:45
  505.2 7.0 %all-reduce.3 = (f32[]{:T(128)}, f32[]{:T(128)}) all-reduce(f32[]{:T(128)} %get-tuple-element.50, f32[]{:T(128)} %get-tuple-element.51), channel_id=1, replica_groups=mesh['line_0'=4,'line_1'=4,'bus'=16] {'line_1'}, use_global_device_ids=true, to_apply=%region_21.24 | all-reduce | flops 2 | bytes 16 | tf_op jit(solution)/shard_map/psum | solution.py:45
  514.9 3.5 all-to-all-start.3
  519.1 5.7 all-to-all-done.3
  526.0 9.2 %all_to_all.34 = f32[16,1,256]{2,1,0:T(1,128)S(1)} all-to-all(f32[16,1,256]{2,1,0:T(1,128)S(1)} %broadcast_in_dim.38), channel_id=1, replica_groups=mesh['line_0'=4,'line_1'=4,'bus'=16] {'line_0','line_1'}, dimensions={0} | all-to-all | bytes 32768 | tf_op jit(solution)/shard_map/all_to_all | solution.py:15
  535.2 17.4 %gather_fusion.4 = f32[3072]{0:T(1024)S(1)} fusion(f32[4097]{0:T(1024)S(1)} %pad_maximum_fusion, s32[3072]{0:T(1024)S(1)} %broadcast_clamp_fusion.1), kind=kCustom, calls=%fused_computation.4 | custom fusion | bytes 36864 | tf_op jit(solution)/shard_map/gather | solution.py:97
  552.6 17.4 %gather_fusion.5 = f32[3072]{0:T(1024)S(1)} fusion(f32[4097]{0:T(1024)S(1)} %pad_maximum_fusion, s32[3072]{0:T(1024)S(1)} %broadcast_clamp_fusion), kind=kCustom, calls=%fused_computation.5 | custom fusion | bytes 36864 | tf_op jit(solution)/shard_map/gather | solution.py:97
  570.2 23.7 %all_to_all.35 = f32[16,1,3072]{2,1,0:T(1,128)S(1)} all-to-all(f32[16,1,3072]{2,1,0:T(1,128)S(1)} %broadcast_in_dim.39), channel_id=1, replica_groups=mesh['line_0'=4,'line_1'=4,'bus'=16] {'bus'}, dimensions={0} | all-to-all | bytes 393216 | tf_op jit(solution)/shard_map/all_to_all | solution.py:15
  594.0 1.2 fusion.29
  595.9 7.5 %all-reduce.7 = (f32[]{:T(128)}, f32[]{:T(128)}) all-reduce(f32[]{:T(128)} %fusion.30, f32[]{:T(128)} %get-tuple-element.60), channel_id=1, replica_groups=mesh['line_0'=4,'line_1'=4,'bus'=16] {'line_0'}, use_global_device_ids=true, to_apply=%region_33.36 | all-reduce | flops 2 | bytes 16 | tf_op jit(solution)/shard_map/pmin | solution.py:67
  603.3 7.6 %all-reduce.5 = (f32[1]{0:T(128)}, f32[1]{0:T(128)}) all-reduce(f32[1]{0:T(128)} %bitcast.97, f32[1]{0:T(128)} %bitcast.96), channel_id=1, replica_groups=mesh['line_0'=4,'line_1'=4,'bus'=16] {'line_1'}, use_global_device_ids=true, to_apply=%region_34.37 | all-reduce | flops 2 | bytes 16 | tf_op jit(solution)/shard_map/pmin | solution.py:67
  610.9 1.9 maximum_multiply_fusion
  (86 shorter events, 13.1 us)
Async XLA Ops:
  26.4 28.3 %copy-start.2 = (s32[2,3072]{1,0:T(2,128)S(1)}, s32[2,3072]{1,0:T(2,128)}, u32[]{:S(2)}) copy-start(s32[2,3072]{1,0:T(2,128)} %param.16) | copy-start | bytes 73732
  26.4 28.3 %copy-start = (f32[3072]{0:T(1024)S(1)}, f32[3072]{0:T(1024)}, u32[]{:S(2)}) copy-start(f32[3072]{0:T(1024)} %param.12) | copy-start | bytes 36868
  26.4 28.3 %copy-start.1 = (f32[3072]{0:T(1024)S(1)}, f32[3072]{0:T(1024)}, u32[]{:S(2)}) copy-start(f32[3072]{0:T(1024)} %param.11) | copy-start | bytes 36868
  44.6 90.6 %all-to-all-start = ((f32[16,1,3072]{2,1,0:T(1,128)}), f32[16,1,3072]{2,1,0:T(1,128)S(1)}, u32[]{:S(2)}, u32[]{:S(2)}) async-start(f32[16,1,3072]{2,1,0:T(1,128)} %broadcast_in_dim.29), calls=%async_computation | async-start | bytes 393216 | tf_op jit(solution)/shard_map/all_to_all | solution.py:15
  54.6 254.8 %all-reduce.11.cloned.1.call-start = ((), (), s32[]{:S(2)}) async-start(), calls=%async_computation.6 | async-start | bytes 8519680
  131.2 4.1 copy-start.5
  194.0 1.2 copy-start.6
  194.0 2.4 copy-start.4
  419.7 19.5 %all-to-all-start.2 = ((f32[16,1,3072]{2,1,0:T(1,128)}), f32[16,1,3072]{2,1,0:T(1,128)S(1)}, u32[]{:S(2)}, u32[]{:S(2)}) async-start(f32[16,1,3072]{2,1,0:T(1,128)} %broadcast_in_dim.35), calls=%async_computation.2 | async-start | bytes 393216 | tf_op jit(solution)/shard_map/all_to_all | solution.py:15
  514.9 9.9 %all-to-all-start.3 = ((f32[16,1,256]{2,1,0:T(1,128)}), f32[16,1,256]{2,1,0:T(1,128)S(1)}, u32[]{:S(2)}, u32[]{:S(2)}) async-start(f32[16,1,256]{2,1,0:T(1,128)} %bitcast.65), calls=%async_computation.3 | async-start | bytes 32768 | tf_op jit(solution)/shard_map/all_to_all | solution.py:61
  595.2 18.2 %copy-start.3 = (f32[3072]{0:T(1024)}, f32[3072]{0:T(1024)S(1)}, u32[]{:S(2)}) copy-start(f32[3072]{0:T(1024)S(1)} %get-tuple-element.148) | copy-start | bytes 36868
Sparse Core Ops, SparseCore 0:
  194.1 115.2 all-reduce.10
where the time goes:
time: 623 us; the launch traced here: 620 us
  other arithmetic  232 us (37%)
  waiting for transfers between devices  129 us (21%)
  local copies, waits for them, and re-layouts  126 us (20%)
  blocking collectives  89.2 us (14%)
  starting transfers between devices  22.8 us (4%)
  between operations  18.4 us (3%)
    unnamed x2, waiting for transfers between devices  113 us
    gather x6, local copies, waits for them, and re-layouts, line_image(): partial_value = padded[own_from] - padded[own_to]  104 us
    all_to_all x3, blocking collectives, from_everyone(): lax.all_to_all(jnp.broadcast_to(x[None], (devices, *x.shape)), axis, 0, 0...  44.4 us
    scatter-add x2, other arithmetic, bus_image(): jax.ops.segment_sum(stacked, slot_from, buses_here + 1)  42.5 us
    scatter-add x2, other arithmetic, bus_image(): jax.ops.segment_sum(stacked, slot_to, buses_here + 1)  41.4 us
    another operation x6, other arithmetic, per_device(): jnp.linalg.cholesky(normal + lax.dynamic_slice_in_dim(fixed_part, first_r...  33.9 us
    pmin x4, blocking collectives, over_axes_2(): x = lax.pmin(x, axis)  30.1 us
    another operation x6, other arithmetic, factor_solve(): lax.linalg.triangular_solve(factor, lower_half, left_side=True, lower=Tru...  19.9 us
  transfers between devices with their start and end apart: 4, of which 3 were waited for; matrix products, arithmetic and copies ran while one was open for 13% of the time, Pallas kernels for 0%

commit v1 on v0

v1 whole, which is shorter than its diff:
```python
import functools

import jax
import jax.numpy as jnp
from jax import lax
from jax.experimental import pallas as pl
from jax.experimental.pallas import tpu as pltpu
from jax.sharding import PartitionSpec as P

damping = 0.99

f32 = jnp.float32
bf16 = jnp.bfloat16
MESH = pl.DeviceIdType.MESH

BS = 256
PLANE = 32
DEPTH = 8
SLOTS = 32
CHUNK = 512


def position():
    li = lax.axis_index("line")
    bi = lax.axis_index("bus")
    z = bi // 2
    c = bi - 2 * z
    return li, z, c


def split3(x):
    high = x.astype(bf16).astype(f32)
    rest = x - high
    middle = rest.astype(bf16).astype(f32)
    return high, middle, rest - middle


def contract_lanes(a, b):
    return lax.dot_general(a, b, (((1,), (1,)), ((), ())), preferred_element_type=f32)


def rows_of(shape):
    return lax.broadcasted_iota(jnp.int32, shape, 0)


def build_selector(selector, place):
    for j in range(place.shape[1] // 256):
        at = slice(256 * j, 256 * (j + 1))
        selector[:, at] = jnp.where(rows_of((BS, 256)) == place[:, at], 1.0, 0.0).astype(bf16)


def to_buses(values, block, selector):
    total = None
    pieces = [piece for v in values for piece in split3(v)]
    for j in range(block.shape[1] // CHUNK):
        at = slice(CHUNK * j, CHUNK * (j + 1))
        here = rows_of((PLANE, CHUNK)) == block[:, at]
        left = jnp.concatenate([jnp.where(here, p[:, at], 0.0).astype(bf16) for p in pieces], axis=0)
        part = contract_lanes(left, selector[:, at])
        total = part if total is None else total + part
    sums = [total[PLANE * k : PLANE * (k + 1)] for k in range(len(pieces))]
    return [sums[3 * q] + sums[3 * q + 1] + sums[3 * q + 2] for q in range(len(values))]


def to_lines(table, block, selector):
    left = jnp.concatenate([p.astype(bf16) for p in split3(table)], axis=0)
    picked = []
    for j in range(block.shape[1] // CHUNK):
        at = slice(CHUNK * j, CHUNK * (j + 1))
        found = jnp.dot(left, selector[:, at], preferred_element_type=f32)
        found = found[0:PLANE] + found[PLANE : 2 * PLANE] + found[2 * PLANE : 3 * PLANE]
        here = rows_of((PLANE, CHUNK)) == block[:, at]
        picked.append(jnp.sum(jnp.where(here, found, 0.0), axis=0, keepdims=True))
    half = len(picked) // 2
    return jnp.concatenate(picked[:half], axis=1) - jnp.concatenate(picked[half:], axis=1)


def endpoint_rows(ends, c, z):
    half = ends.shape[1] // 2
    at = pl.ds(pl.multiple_of(c * half, half), half)
    start, end = ends[0:1, at], ends[1:2, at]
    both = jnp.concatenate([start, end], axis=1)
    return start, end, both & (BS - 1), (both >> 8) - PLANE * z


def greet(li, z, c):
    barrier = pltpu.get_barrier_semaphore()
    mine = 2 * li + c

    def plane(k, carry):
        s = lax.rem(mine + k, PLANE)
        pl.semaphore_signal(barrier, 1, device_id=(s // 2, 2 * z + lax.rem(s, 2)), device_id_type=MESH)
        return carry

    def depth(k, carry):
        pl.semaphore_signal(barrier, 1, device_id=(li, 2 * lax.rem(z + k, DEPTH) + c), device_id_type=MESH)
        return carry

    lax.fori_loop(1, PLANE, plane, 0)
    lax.fori_loop(1, DEPTH, depth, 0)


def greeted():
    pl.semaphore_wait(pltpu.get_barrier_semaphore(), PLANE - 1 + DEPTH - 1)


def send_plane(pick, home, slot, recv, send_sem, recv_sem, li, z, c):
    mine = 2 * li + c

    def body(k, carry):
        s = lax.rem(mine + k, PLANE)
        l2, c2 = s // 2, lax.rem(s, 2)
        pltpu.make_async_remote_copy(
            pick(c2 * 16 + l2), recv.at[slot], send_sem, recv_sem, device_id=(l2, 2 * z + c2), device_id_type=MESH
        ).start()
        return carry

    lax.fori_loop(1, PLANE, body, 0)
    pltpu.make_async_copy(home, recv.at[slot], recv_sem).start()


def send_depth(src, recv, send_sem, recv_sem, li, z, c):
    def body(k, carry):
        pltpu.make_async_remote_copy(
            src,
            recv.at[z],
            send_sem,
            recv_sem,
            device_id=(li, 2 * lax.rem(z + k, DEPTH) + c),
            device_id_type=MESH,
        ).start()
        return carry

    lax.fori_loop(1, DEPTH, body, 0)
    pltpu.make_async_copy(src, recv.at[z], recv_sem).start()


def wait_bytes(ref, sem):
    pltpu.make_async_copy(ref, ref, sem).wait()


def sum_slots(recv, at):
    total = recv[0, :, at]
    for s in range(1, recv.shape[0]):
        total = total + recv[s, :, at]
    return total


def front_kernel(
    primal, slacks, cost, ends, bus_dual, demand, fixed,
    m_out, rhs_out, third_out, dual_out, scal_out,
    selector, partner, msg, msg_in, diff, diff_in, part, part_in, block_in,
    fixed_sem, pair_sem, msg_sem, diff_sem, part_sem,
):
    li, z, c = position()
    own = pltpu.make_async_copy(fixed.at[li], block_in, fixed_sem)
    own.start()
    greet(li, z, c)
    half = primal.shape[1] // 2
    mine = pl.ds(pl.multiple_of(c * half, half), half)
    x, s = primal[:, mine], slacks[:, mine]
    start, end, place, block = endpoint_rows(ends, c, z)
    build_selector(selector, place)
    scaling = x / s
    inverse = 1.0 / s
    gap = jnp.sum(x * s, axis=1, keepdims=True)

    first = block[:, :half]
    owner = jnp.where((start >> 8) == (end >> 8), first, -1)
    order = jnp.where(rows_of((256, 256)) < lax.broadcasted_iota(jnp.int32, (256, 256), 1), 1.0, 0.0).astype(bf16)
    carry = jnp.zeros((PLANE, 1), f32)
    packed = None
    shift = (SLOTS * lax.rem(2 * li + c, 128 // SLOTS)).astype(f32)
    values = [place[:, :half].astype(f32), place[:, half:].astype(f32), *split3(scaling)]
    for j in range(half // 256):
        at = slice(256 * j, 256 * (j + 1))
        here = rows_of((PLANE, 256)) == owner[:, at]
        marks = jnp.where(here, 1.0, 0.0)
        rank = jnp.dot(marks.astype(bf16), order, preferred_element_type=f32) + carry
        carry = carry + jnp.sum(marks, axis=1, keepdims=True)
        rank = jnp.sum(jnp.where(here, rank, 0.0), axis=0, keepdims=True)
        code = jnp.where(rank < SLOTS, rank + shift, -1.0)
        slots = jnp.where(rows_of((128, 256)).astype(f32) == code, 1.0, 0.0).astype(bf16)
        left = jnp.concatenate([jnp.where(here, v[:, at], 0.0).astype(bf16) for v in values], axis=0)
        piece = contract_lanes(left, slots)
        packed = piece if packed is None else packed + piece
    most = jnp.max(carry, axis=0, keepdims=True)
    packed = [packed[PLANE * k : PLANE * (k + 1)] for k in range(5)]

    ends_sum, third = to_buses(
        [jnp.concatenate([scaling, scaling], axis=1), jnp.concatenate([inverse, -inverse], axis=1)], block, selector
    )
    whole = jnp.concatenate(
        [ends_sum, third, packed[0], packed[1], packed[2] + packed[3] + packed[4], jnp.broadcast_to(gap, (PLANE, 128))],
        axis=1,
    )
    for b in range(PLANE):
        msg[b] = whole[b : b + 1]

    greeted()
    pair = pltpu.make_async_remote_copy(
        bus_dual, partner, pair_sem.at[0], pair_sem.at[1], device_id=(li, 2 * z + 1 - c), device_id_type=MESH
    )
    pair.start()
    at_home = c * 16 + li
    send_plane(lambda b: msg.at[b], msg.at[at_home], 2 * li + c, msg_in, msg_sem.at[0], msg_sem.at[1], li, z, c)

    pair.wait()
    mine_dual = jnp.concatenate([bus_dual[:, BS * k : BS * (k + 1)] for k in range(16)], axis=0)
    other_dual = jnp.concatenate([partner[:, BS * k : BS * (k + 1)] for k in range(16)], axis=0)
    table = jnp.concatenate(
        [jnp.where(c == 0, mine_dual, other_dual), jnp.where(c == 0, other_dual, mine_dual)], axis=0
    )
    diff[:, :half] = to_lines(table, block, selector)
    diff[:, half:] = jnp.broadcast_to(most, (1, 128))
    send_depth(diff, diff_in, diff_sem.at[0], diff_sem.at[1], li, z, c)

    wait_bytes(diff_in, diff_sem.at[1])
    dual_res = cost[:, mine] - sum_slots(diff_in, slice(0, half)) - s
    dual_out[...] = dual_res
    most = diff_in[0, :, half:]
    for k in range(1, DEPTH):
        most = jnp.maximum(most, diff_in[k, :, half:])
    flow = scaling * dual_res
    (right,) = to_buses([jnp.concatenate([flow, -flow], axis=1)], block, selector)
    whole = jnp.concatenate([right, jnp.broadcast_to(most, (PLANE, 128))], axis=1)
    for b in range(PLANE):
        part[b] = whole[b : b + 1]
    send_plane(lambda b: part.at[b], part.at[at_home], 2 * li + c, part_in, part_sem.at[0], part_sem.at[1], li, z, c)

    wait_bytes(msg_in, msg_sem.at[1])
    sums = sum_slots(msg_in, slice(0, 512))
    third_out[...] = sums[:, 256:]
    group = 128 // SLOTS

    def candidates(g, at):
        return sum(msg_in[group * g + k, :, at] for k in range(1, group)) + msg_in[group * g, :, at]

    total = None
    near = rows_of((BS, 128)).astype(f32)
    for g in range(PLANE // group):
        p, q, d = (candidates(g, slice(512 + 128 * k, 640 + 128 * k)) for k in range(3))
        from_here, to_here = near == p, near == q
        right_side = jnp.concatenate(
            [jnp.where(to_here, 1.0, 0.0).astype(bf16), jnp.where(from_here, 1.0, 0.0).astype(bf16)], axis=1
        )
        for piece in split3(d):
            left = jnp.concatenate(
                [jnp.where(from_here, piece, 0.0).astype(bf16), jnp.where(to_here, piece, 0.0).astype(bf16)], axis=1
            )
            add = contract_lanes(left, right_side)
            total = add if total is None else total + add
    own.wait()
    diagonal = rows_of((BS, BS)) == lax.broadcasted_iota(jnp.int32, (BS, BS), 1)
    m_out[...] = block_in[...] + jnp.where(diagonal, sums[:, :256], 0.0) - total

    wait_bytes(part_in, part_sem.at[1])
    rhs_out[...] = demand[:, pl.ds(pl.multiple_of(li * BS, BS), BS)] + sum_slots(part_in, slice(0, 256))
    most = part_in[0, :, 256:]
    for k in range(1, PLANE):
        most = jnp.maximum(most, part_in[k, :, 256:])
    scal_out[0:1] = sum_slots(msg_in, slice(896, 1024))
    scal_out[1:2] = most
    wait_bytes(msg_in.at[pl.ds(0, PLANE - 1)], msg_sem.at[0])
    wait_bytes(diff_in.at[pl.ds(0, DEPTH - 1)], diff_sem.at[0])
    wait_bytes(part_in.at[pl.ds(0, PLANE - 1)], part_sem.at[0])


def invert_kernel(m_ref, out_ref):
    n = m_ref.shape[0]
    w = 32
    out_ref[...] = m_ref[...]
    lane = lax.broadcasted_iota(jnp.int32, (w, 128), 1)
    row = rows_of((w, 128))
    lane1 = lax.broadcasted_iota(jnp.int32, (1, 128), 1)

    def panel(_, carry):
        ra, rb = out_ref[0:w, 0:128], out_ref[0:w, 128:256]
        for sub in range(w // 8):
            cols = [jnp.broadcast_to(ra[:, j : j + 1], (w, 128)) for j in range(8 * sub, 8 * sub + 8)]
            for k in range(8):
                r = 8 * sub + k
                ck = cols[k]
                rp = 1.0 / ck[r : r + 1, :]
                pa = jnp.where(lane1 == r, 1.0, ra[r : r + 1, :]) * rp
                pb = rb[r : r + 1, :] * rp
                here = row == r
                ra = jnp.where(here, pa, jnp.where(lane == r, 0.0, ra) - ck * pa)
                rb = jnp.where(here, pb, rb - ck * pb)
                for j in range(k + 1, 8):
                    cr = cols[j][r : r + 1, :] * rp
                    cols[j] = jnp.where(here, cr, cols[j] - ck * cr)
        top = jnp.concatenate([ra, rb], axis=1)
        rest = out_ref[w:n, :]
        wide = jnp.concatenate([top, jnp.zeros((128 - w, n), f32)], axis=0)
        update = jnp.dot(rest[:, 0:128], wide, precision=lax.Precision.HIGHEST, preferred_element_type=f32)
        lanes = lax.broadcasted_iota(jnp.int32, (n - w, n), 1)
        rest = jnp.where(lanes < w, 0.0, rest) - update
        out_ref[0 : n - w, :] = pltpu.roll(rest, n - w, 1)
        out_ref[n - w : n, :] = pltpu.roll(top, n - w, 1)
        return carry

    lax.fori_loop(0, n // w, panel, 0)


def longest_step(now, step):
    return jnp.min(now / jnp.maximum(-step, now), axis=1, keepdims=True)


def back_kernel(
    total_lines,
    primal, slacks, ends, inverse, rhs, third, dual, scal,
    step_primal, step_slack, step_dual, lengths,
    selector, solved, solved_in, diff, diff_in, part, part_in,
    solved2, solved2_in, diff2, diff2_in, final, final_in, last, last_in,
    solved_sem, diff_sem, part_sem, solved2_sem, diff2_sem, last_sem, final_sem,
):
    li, z, c = position()
    greet(li, z, c)
    half = primal.shape[1] // 2
    mine = pl.ds(pl.multiple_of(c * half, half), half)
    x, s, dual_res = primal[:, mine], slacks[:, mine], dual[...]
    _, _, place, block = endpoint_rows(ends, c, z)
    build_selector(selector, place)
    scaling = x / s
    at_home = c * 16 + li
    gap_total = scal[0:1, :]

    def solve(right):
        wide = jnp.broadcast_to(right, (8, BS))
        return jnp.dot(wide, inverse[...], precision=lax.Precision.HIGHEST, preferred_element_type=f32)[0:1]

    solved[...] = solve(rhs[...])
    greeted()
    send_plane(lambda b: solved, solved, at_home, solved_in, solved_sem.at[0], solved_sem.at[1], li, z, c)
    wait_bytes(solved_in, solved_sem.at[1])
    table = jnp.concatenate([solved_in[b] for b in range(PLANE)], axis=0)
    diff[...] = to_lines(table, block, selector)
    send_depth(diff, diff_in, diff_sem.at[0], diff_sem.at[1], li, z, c)
    wait_bytes(diff_in, diff_sem.at[1])
    affine_slack = dual_res - sum_slots(diff_in, slice(0, half))
    affine_primal = -x - scaling * affine_slack
    cross = affine_primal * affine_slack
    extra = cross / s
    (sums,) = to_buses([jnp.concatenate([extra, -extra], axis=1)], block, selector)
    lane1 = lax.broadcasted_iota(jnp.int32, (1, 128), 1)
    scalars = [
        longest_step(x, affine_primal),
        longest_step(s, affine_slack),
        jnp.sum(affine_primal * s, axis=1, keepdims=True),
        jnp.sum(x * affine_slack, axis=1, keepdims=True),
        jnp.sum(cross, axis=1, keepdims=True),
    ]
    row = jnp.zeros((1, 128), f32)
    for k, value in enumerate(scalars):
        row = jnp.where(lane1 == k, value, row)
    whole = jnp.concatenate([sums, jnp.broadcast_to(row, (PLANE, 128))], axis=1)
    for b in range(PLANE):
        part[b] = whole[b : b + 1]
    send_plane(lambda b: part.at[b], part.at[at_home], 2 * li + c, part_in, part_sem.at[0], part_sem.at[1], li, z, c)
    wait_bytes(part_in, part_sem.at[1])
    added = sum_slots(part_in, slice(0, 384))
    least = part_in[0, :, 256:384]
    for k in range(1, PLANE):
        least = jnp.minimum(least, part_in[k, :, 256:384])
    take_p, take_d = least[:, 0:1], least[:, 1:2]
    tail = added[:, 256:384]
    gap0 = gap_total[:, 0:1]
    gap_affine = gap0 + take_p * tail[:, 2:3] + take_d * tail[:, 3:4] + take_p * take_d * tail[:, 4:5]
    ratio = gap_affine / gap0
    aim = ratio * ratio * ratio * (gap0 / total_lines)
    solved2[...] = solve(rhs[...] - aim * third[...] + added[:, :256])
    send_plane(lambda b: solved2, solved2, at_home, solved2_in, solved2_sem.at[0], solved2_sem.at[1], li, z, c)
    wait_bytes(solved2_in, solved2_sem.at[1])
    table = jnp.concatenate([solved2_in[b] for b in range(PLANE)], axis=0)
    diff2[...] = to_lines(table, block, selector)
    send_depth(diff2, diff2_in, diff2_sem.at[0], diff2_sem.at[1], li, z, c)
    for b in range(16):
        step_dual[:, BS * b : BS * (b + 1)] = solved2_in[16 * c + b]
    wait_bytes(diff2_in, diff2_sem.at[1])
    slack = dual_res - sum_slots(diff2_in, slice(0, half))
    primal_step = (aim - x * s - cross) / s - scaling * slack
    row = jnp.where(lane1 == 0, longest_step(x, primal_step), longest_step(s, slack))
    last[...] = row
    final[0:1] = primal_step
    final[1:2] = slack
    step_primal[:, mine] = primal_step
    step_slack[:, mine] = slack
    send_plane(lambda b: last, last, 2 * li + c, last_in, last_sem.at[0], last_sem.at[1], li, z, c)
    pair = pltpu.make_async_remote_copy(
        final, final_in, final_sem.at[0], final_sem.at[1], device_id=(li, 2 * z + 1 - c), device_id_type=MESH
    )
    pair.start()
    pair.wait()
    other = pl.ds(pl.multiple_of((1 - c) * half, half), half)
    step_primal[:, other] = final_in[0:1]
    step_slack[:, other] = final_in[1:2]
    wait_bytes(last_in, last_sem.at[1])
    least = last_in[0]
    for k in range(1, PLANE):
        least = jnp.minimum(least, last_in[k])
    lengths[...] = damping * least
    wait_bytes(solved_in.at[pl.ds(0, PLANE - 1)], solved_sem.at[0])
    wait_bytes(diff_in.at[pl.ds(0, DEPTH - 1)], diff_sem.at[0])
    wait_bytes(part_in.at[pl.ds(0, PLANE - 1)], part_sem.at[0])
    wait_bytes(solved2_in.at[pl.ds(0, PLANE - 1)], solved2_sem.at[0])
    wait_bytes(diff2_in.at[pl.ds(0, DEPTH - 1)], diff2_sem.at[0])
    wait_bytes(last_in.at[pl.ds(0, PLANE - 1)], last_sem.at[0])


def vmem(n):
    return [pl.BlockSpec(memory_space=pltpu.VMEM)] * n


def struct(*shape):
    return jax.ShapeDtypeStruct(shape, f32)


def scattered_block(primal, slacks, endpoints, fixed_part):
    blocks_here, block_size = fixed_part.shape[0], fixed_part.shape[1]
    buses_here = blocks_here * block_size
    scaling = primal / slacks
    local = endpoints - lax.axis_index("bus") * buses_here
    own_from, own_to = jnp.where((local >= 0) & (local < buses_here), local, buses_here)
    same_block = endpoints[0] // block_size == endpoints[1] // block_size
    crossing = jnp.where(same_block, -scaling, jnp.zeros_like(scaling))
    rows = jnp.concatenate([own_from, own_to, own_from, own_to])
    columns = jnp.concatenate([own_from, own_to, own_to, own_from]) % block_size
    values = jnp.concatenate([scaling, scaling, crossing, crossing])
    flat = jnp.zeros((buses_here * block_size,), f32).at[rows * block_size + columns].add(values, mode="drop")
    lines = lax.psum_scatter(flat.reshape(-1, 128), "line", tiled=True)
    mine = lax.dynamic_index_in_dim(fixed_part, lax.axis_index("line"), 0, keepdims=False)
    return mine + lines.reshape(block_size, block_size)


def per_device(primal, slacks, line_cost, bus_dual, demand, endpoints, fixed_part):
    lines_here, buses_here = primal.shape[0], bus_dual.shape[0]
    half = lines_here // 2
    total_lines = lines_here * lax.axis_size("line")
    dma = pltpu.SemaphoreType.DMA
    x, s = primal.reshape(1, -1), slacks.reshape(1, -1)
    fast, rhs, third, dual, scal = pl.pallas_call(
        front_kernel,
        out_shape=(struct(BS, BS), struct(1, BS), struct(1, BS), struct(1, half), struct(2, 128)),
        in_specs=vmem(6) + [pl.BlockSpec(memory_space=pl.ANY)],
        out_specs=tuple(vmem(5)),
        scratch_shapes=[
            pltpu.VMEM((BS, lines_here), bf16),
            pltpu.VMEM((1, buses_here), f32),
            pltpu.VMEM((PLANE, 1, 1024), f32),
            pltpu.VMEM((PLANE, 1, 1024), f32),
            pltpu.VMEM((1, half + 128), f32),
            pltpu.VMEM((DEPTH, 1, half + 128), f32),
            pltpu.VMEM((PLANE, 1, 384), f32),
            pltpu.VMEM((PLANE, 1, 384), f32),
            pltpu.VMEM((BS, BS), f32),
            dma,
            dma((2,)),
            dma((2,)),
            dma((2,)),
            dma((2,)),
        ],
        compiler_params=pltpu.CompilerParams(collective_id=0, has_side_effects=True),
        name="front",
    )(x, s, line_cost.reshape(1, -1), endpoints, bus_dual.reshape(1, -1), demand.reshape(1, -1), fixed_part)
    normal = lax.cond(
        scal[1, 0] > SLOTS,
        lambda: scattered_block(primal, slacks, endpoints, fixed_part),
        lambda: fast,
    )
    inverse = pl.pallas_call(
        invert_kernel, out_shape=struct(BS, BS), in_specs=vmem(1), out_specs=vmem(1)[0], name="invert"
    )(normal)
    step_primal, step_slack, step_dual, lengths = pl.pallas_call(
        functools.partial(back_kernel, float(total_lines)),
        out_shape=(struct(1, lines_here), struct(1, lines_here), struct(1, buses_here), struct(1, 128)),
        in_specs=vmem(8),
        out_specs=tuple(vmem(4)),
        scratch_shapes=[
            pltpu.VMEM((BS, lines_here), bf16),
            pltpu.VMEM((1, BS), f32),
            pltpu.VMEM((PLANE, 1, BS), f32),
            pltpu.VMEM((1, half), f32),
            pltpu.VMEM((DEPTH, 1, half), f32),
            pltpu.VMEM((PLANE, 1, 384), f32),
            pltpu.VMEM((PLANE, 1, 384), f32),
            pltpu.VMEM((1, BS), f32),
            pltpu.VMEM((PLANE, 1, BS), f32),
            pltpu.VMEM((1, half), f32),
            pltpu.VMEM((DEPTH, 1, half), f32),
            pltpu.VMEM((2, half), f32),
            pltpu.VMEM((2, half), f32),
            pltpu.VMEM((1, 128), f32),
            pltpu.VMEM((PLANE, 1, 128), f32),
        ]
        + [dma((2,))] * 7,
        compiler_params=pltpu.CompilerParams(collective_id=1, has_side_effects=True),
        name="back",
    )(x, s, endpoints, inverse, rhs, third, dual, scal)
    return step_primal.reshape(-1), step_slack.reshape(-1), step_dual.reshape(-1), lengths[0, :2]


def solution(mesh):
    in_specs = (P("line"), P("line"), P("line"), P("bus"), P("bus"), P(None, "line"), P("bus", None, None))
    out_specs = (P("line"), P("line"), P("bus"), P())
    return jax.shard_map(per_device, mesh=mesh, in_specs=in_specs, out_specs=out_specs, check_vma=False)
```

time: 623 us -> 93.5 us (0.15)
  other arithmetic: 232 us -> 0 us
  waiting for transfers between devices: 129 us -> 0 us
  local copies, waits for them, and re-layouts: 126 us -> 6.23 us
  blocking collectives: 89.2 us -> 0 us
  Pallas kernels: 0 us -> 72 us
  starting transfers between devices: 22.8 us -> 0 us
    scatter-add x8 -> x0, other arithmetic: 160 us -> none  [the longest x2 42.5 us: bus_image(): jax.ops.segment_sum(stacked, slot_from, buses_here + 1)]
    unnamed x2 -> x0, waiting for transfers between devices: 113 us -> none
    gather x6 -> x0, local copies, waits for them, and re-layouts: 104 us -> none  [line_image(): partial_value = padded[own_from] - padded[own_to]]
    pallas_call x0 -> x3, Pallas kernels: none -> 72 us  [the longest x1 37.6 us: per_device(): pl.pallas_call(functools.partial(back_kernel, float(total_lines)), out_sh...]
    another operation x12 -> x0, other arithmetic: 53.9 us -> none  [the longest x6 33.9 us: per_device(): jnp.linalg.cholesky(normal + lax.dynamic_slice_in_dim(fixed_part, first_r...]
    all_to_all x3 -> x0, blocking collectives: 44.4 us -> none  [from_everyone(): lax.all_to_all(jnp.broadcast_to(x[None], (devices, *x.shape)), axis, 0, 0...]
    pmin x4 -> x0, blocking collectives: 30.1 us -> none  [over_axes_2(): x = lax.pmin(x, axis)]
    all_to_all x3 -> x0, starting transfers between devices: 22.8 us -> none  [the longest x2 19.3 us: from_everyone(): lax.all_to_all(jnp.broadcast_to(x[None], (devices, *x.shape)), axis, 0, 0...]
  transfers between devices with their start and end apart: 4 -> 0, of which waited for: 3 -> 0; matrix products, arithmetic and copies ran while one was open for 13% -> 0% of each run, Pallas kernels for 0% -> 0%
where the time goes in v1:
time: 93.5 us; the launch traced here: 93 us
  Pallas kernels  72 us (77%)
  between operations  14.7 us (16%)
  local copies, waits for them, and re-layouts  6.23 us (7%)
    pallas_call x1, Pallas kernels, per_device(): pl.pallas_call(functools.partial(back_kernel, float(total_lines)), out_sh...  37.6 us
    pallas_call x1, Pallas kernels, per_device(): pl.pallas_call(front_kernel, out_shape=(struct(BS, BS), struct(1, BS), st...  24.4 us
    pallas_call x1, Pallas kernels, per_device(): pl.pallas_call(invert_kernel, out_shape=struct(BS, BS), in_specs=vmem(1),...  10 us
    unnamed x9, local copies, waits for them, and re-layouts  3.95 us

profile of v1, /device:TPU:1, one launch (start us, length us, event | category | flops | bytes accessed | tf_op | source)
XLA Modules:
  0.0 93.0 jit_solution(9810935654247181153)
XLA Ops:
  7.2 0.0 copy-start
  7.2 0.0 copy-start.2
  7.2 0.0 copy-start.1
  7.2 24.4 %front.1 = (f32[256,256]{1,0:T(8,128)S(1)}, f32[1,256]{1,0:T(1,128)}, f32[1,256]{1,0:T(1,128)}, f32[1,1536]{1,0:T(1,128)}, f32[2,128]{1,0:T(2,128)}) custom-call(f32[1,3072]{1,0:T(1,128)} %bitcast.22, f32[1,3072]{1,0:T(1,128)} %bitcast.24, f32[1,3072]{1,0:T(1,128)} %bitcast.32, s32[2,3072]{1,0:T(2,128)} %ends.3, f32[1,4096]{1,0:T(1,128)} %bitcast.29, ...), custom_call_target="tpu_custom_call" | custom-call | tf_op jit(solution)/shard_map/front/pallas_call | solution.py:442
  31.6 1.2 %slice.12 = f32[1,1]{1,0:T(1,128)} slice(f32[2,128]{1,0:T(2,128)} %get-tuple-element.29.scal), slice={[1:2], [0:1]} | slice | bytes 8 | tf_op jit(solution)/shard_map/slice | solution.py:467
  33.4 0.0 copy-done
  33.4 0.0 copy-done.2
  33.4 0.0 copy-done.1
  33.5 10.0 %invert.1.inverse = f32[256,256]{1,0:T(8,128)} custom-call(f32[256,256]{1,0:T(8,128)S(1)} %get-tuple-element.52.m_ref), custom_call_target="tpu_custom_call" | custom-call | tf_op jit(solution)/shard_map/invert/pallas_call | solution.py:471
  43.5 37.6 %back.1 = (f32[1,3072]{1,0:T(1,128)}, f32[1,3072]{1,0:T(1,128)}, f32[1,4096]{1,0:T(1,128)}, f32[1,128]{1,0:T(1,128)}) custom-call(f32[1,3072]{1,0:T(1,128)S(1)} %bitcast.23, f32[1,3072]{1,0:T(1,128)S(1)} %bitcast.25, s32[2,3072]{1,0:T(2,128)S(1)} %copy-done, f32[256,256]{1,0:T(8,128)} %invert.1.inverse, f32[1,256]{1,0:T(1,128)} %get-tuple-element.31.rhs, ...), custom_call_target="tpu_custom_call" | custom-call | tf_op jit(solution)/shard_map/back/pallas_call | solution.py:474
  81.1 1.1 %slice_bitcast_fusion.2 = f32[2]{0:T(128)} fusion(f32[1,128]{1,0:T(1,128)} %get-tuple-element.37), kind=kLoop, calls=%fused_computation.32 | loop fusion | bytes 16 | tf_op jit(solution)/shard_map/squeeze | solution.py:500
  82.2 1.3 %copy.16 = f32[3072]{0:T(1024)} copy(f32[3072]{0:T(1024)} %bitcast.34) | data formatting | bytes 24576
  83.5 1.3 %copy.17 = f32[3072]{0:T(1024)} copy(f32[3072]{0:T(1024)} %bitcast.33) | data formatting | bytes 24576
  84.8 1.3 %copy.18 = f32[4096]{0:T(1024)} copy(f32[4096]{0:T(1024)} %bitcast.31) | data formatting | bytes 32768
  (1 shorter events, 0.0 us)
Async XLA Ops:
  7.2 26.3 %copy-start = (s32[2,3072]{1,0:T(2,128)S(1)}, s32[2,3072]{1,0:T(2,128)}, u32[]{:S(2)}) copy-start(s32[2,3072]{1,0:T(2,128)} %ends.3) | copy-start | bytes 73732
  7.2 26.3 %copy-start.2 = (f32[3072]{0:T(1024)S(1)}, f32[3072]{0:T(1024)}, u32[]{:S(2)}) copy-start(f32[3072]{0:T(1024)} %param.10) | copy-start | bytes 36868
  7.2 26.3 %copy-start.1 = (f32[3072]{0:T(1024)S(1)}, f32[3072]{0:T(1024)}, u32[]{:S(2)}) copy-start(f32[3072]{0:T(1024)} %param.9) | copy-start | bytes 36868

commit v2 on v1

--- a/solution.py
+++ b/solution.py
@@ -428,9 +428,16 @@
     columns = jnp.concatenate([own_from, own_to, own_to, own_from]) % block_size
     values = jnp.concatenate([scaling, scaling, crossing, crossing])
     flat = jnp.zeros((buses_here * block_size,), f32).at[rows * block_size + columns].add(values, mode="drop")
-    lines = lax.psum_scatter(flat.reshape(-1, 128), "line", tiled=True)
+    tiles = lax.all_to_all(flat.reshape(blocks_here, block_size, block_size), "line", 0, 0, tiled=True)
     mine = lax.dynamic_index_in_dim(fixed_part, lax.axis_index("line"), 0, keepdims=False)
-    return mine + lines.reshape(block_size, block_size)
+    return mine + jnp.sum(tiles, axis=0)
+
+
+def hand_over(step_primal, step_slack, step_dual, lengths, primal_out, slack_out, dual_out, lengths_out):
+    primal_out[...] = step_primal[...]
+    slack_out[...] = step_slack[...]
+    dual_out[...] = step_dual[...]
+    lengths_out[...] = lengths[:, 0:2]
 
 
 def per_device(primal, slacks, line_cost, bus_dual, demand, endpoints, fixed_part):
@@ -497,7 +504,14 @@
         compiler_params=pltpu.CompilerParams(collective_id=1, has_side_effects=True),
         name="back",
     )(x, s, endpoints, inverse, rhs, third, dual, scal)
-    return step_primal.reshape(-1), step_slack.reshape(-1), step_dual.reshape(-1), lengths[0, :2]
+    outputs = pl.pallas_call(
+        hand_over,
+        out_shape=(struct(1, lines_here), struct(1, lines_here), struct(1, buses_here), struct(1, 2)),
+        in_specs=vmem(4),
+        out_specs=tuple(vmem(4)),
+        name="hand_over",
+    )(step_primal, step_slack, step_dual, lengths)
+    return tuple(out.reshape(-1) for out in outputs)
 
 
 def solution(mesh):

time: 93.5 us -> 76.2 us (0.81)
  between operations: 14.7 us -> 1.36 us
  local copies, waits for them, and re-layouts: 6.23 us -> 1.21 us
  Pallas kernels: 72 us -> 73.4 us
    unnamed x9 -> x6, local copies, waits for them, and re-layouts: 3.95 us -> 0.01 us
    pallas_call x0 -> x1, Pallas kernels: none -> 1.37 us  [per_device(): pl.pallas_call(hand_over, out_shape=(struct(1, lines_here), struct(1, lin...]
    squeeze x1 -> x0, local copies, waits for them, and re-layouts: 1.12 us -> none  [per_device(): lengths[0, :2]]
where the time goes in v2:
time: 76.2 us; the launch traced here: 76 us
  Pallas kernels  73.4 us (96%)
  between operations  1.36 us (2%)
  local copies, waits for them, and re-layouts  1.21 us (2%)
    pallas_call x1, Pallas kernels, per_device(): pl.pallas_call(functools.partial(back_kernel, float(total_lines)), out_sh...  37.6 us
    pallas_call x1, Pallas kernels, per_device(): pl.pallas_call(front_kernel, out_shape=(struct(BS, BS), struct(1, BS), st...  24.4 us
    pallas_call x1, Pallas kernels, per_device(): pl.pallas_call(invert_kernel, out_shape=struct(BS, BS), in_specs=vmem(1),...  10 us

profile of v2, /device:TPU:1, one launch (start us, length us, event | category | flops | bytes accessed | tf_op | source)
XLA Modules:
  0.0 76.0 jit_solution(3774902636067864185)
XLA Ops:
  0.6 0.0 copy-start
  0.6 0.0 copy-start.2
  0.7 0.0 copy-start.1
  0.7 24.4 %front.1 = (f32[256,256]{1,0:T(8,128)S(1)}, f32[1,256]{1,0:T(1,128)}, f32[1,256]{1,0:T(1,128)}, f32[1,1536]{1,0:T(1,128)}, f32[2,128]{1,0:T(2,128)}) custom-call(f32[1,3072]{1,0:T(1,128)} %bitcast.19, f32[1,3072]{1,0:T(1,128)} %bitcast.21, f32[1,3072]{1,0:T(1,128)} %bitcast.28, s32[2,3072]{1,0:T(2,128)} %ends.3, f32[1,4096]{1,0:T(1,128)} %bitcast.26, ...), custom_call_target="tpu_custom_call" | custom-call | tf_op jit(solution)/shard_map/front/pallas_call | solution.py:449
  25.1 1.2 %slice.9 = f32[1,1]{1,0:T(1,128)} slice(f32[2,128]{1,0:T(2,128)} %get-tuple-element.33.scal), slice={[1:2], [0:1]} | slice | bytes 8 | tf_op jit(solution)/shard_map/slice | solution.py:474
  26.9 0.0 copy-done
  26.9 0.0 copy-done.2
  26.9 0.0 copy-done.1
  27.0 10.0 %invert.1.inverse = f32[256,256]{1,0:T(8,128)} custom-call(f32[256,256]{1,0:T(8,128)S(1)} %get-tuple-element.52.m_ref), custom_call_target="tpu_custom_call" | custom-call | tf_op jit(solution)/shard_map/invert/pallas_call | solution.py:478
  37.0 37.6 %back.1 = (f32[1,3072]{1,0:T(1,128)}, f32[1,3072]{1,0:T(1,128)}, f32[1,4096]{1,0:T(1,128)}, f32[1,128]{1,0:T(1,128)}) custom-call(f32[1,3072]{1,0:T(1,128)S(1)} %bitcast.20, f32[1,3072]{1,0:T(1,128)S(1)} %bitcast.22, s32[2,3072]{1,0:T(2,128)S(1)} %copy-done, f32[256,256]{1,0:T(8,128)} %invert.1.inverse, f32[1,256]{1,0:T(1,128)} %get-tuple-element.35.rhs, ...), custom_call_target="tpu_custom_call" | custom-call | tf_op jit(solution)/shard_map/back/pallas_call | solution.py:481
  74.6 1.4 %hand_over.1 = (f32[1,3072]{1,0:T(1,128)}, f32[1,3072]{1,0:T(1,128)}, f32[1,4096]{1,0:T(1,128)}, f32[1,2]{1,0:T(1,128)}) custom-call(f32[1,3072]{1,0:T(1,128)} %get-tuple-element.38.step_primal, f32[1,3072]{1,0:T(1,128)} %get-tuple-element.39.step_slack, f32[1,4096]{1,0:T(1,128)} %get-tuple-element.40.step_dual, f32[1,128]{1,0:T(1,128)} %get-tuple-element.41.lengths), custom_call_target="tpu_custom_call" | custom-call | tf_op jit(solution)/shard_map/hand_over/pallas_call | solution.py:507
  (1 shorter events, 0.0 us)
Async XLA Ops:
  0.6 26.3 %copy-start = (s32[2,3072]{1,0:T(2,128)S(1)}, s32[2,3072]{1,0:T(2,128)}, u32[]{:S(2)}) copy-start(s32[2,3072]{1,0:T(2,128)} %ends.3) | copy-start | bytes 73732
  0.6 26.3 %copy-start.2 = (f32[3072]{0:T(1024)S(1)}, f32[3072]{0:T(1024)}, u32[]{:S(2)}) copy-start(f32[3072]{0:T(1024)} %param.10) | copy-start | bytes 36868
  0.7 26.3 %copy-start.1 = (f32[3072]{0:T(1024)S(1)}, f32[3072]{0:T(1024)}, u32[]{:S(2)}) copy-start(f32[3072]{0:T(1024)} %param.9) | copy-start | bytes 36868

commit v3 on v2

v3 whole, which is shorter than its diff:
```python
import functools

import jax
import jax.numpy as jnp
from jax import lax
from jax.experimental import pallas as pl
from jax.experimental.pallas import tpu as pltpu
from jax.sharding import PartitionSpec as P

damping = 0.99

f32 = jnp.float32
bf16 = jnp.bfloat16
MESH = pl.DeviceIdType.MESH

BS = 256
PLANE = 32
DEPTH = 8
SLOTS = 32
CHUNK = 512


def position():
    li = lax.axis_index("line")
    bi = lax.axis_index("bus")
    z = bi // 2
    c = bi - 2 * z
    return li, z, c


def split3(x):
    high = x.astype(bf16).astype(f32)
    rest = x - high
    middle = rest.astype(bf16).astype(f32)
    return high, middle, rest - middle


def contract_lanes(a, b):
    return lax.dot_general(a, b, (((1,), (1,)), ((), ())), preferred_element_type=f32)


def rows_of(shape):
    return lax.broadcasted_iota(jnp.int32, shape, 0)


def build_selector(selector, place):
    for j in range(place.shape[1] // 256):
        at = slice(256 * j, 256 * (j + 1))
        selector[:, at] = jnp.where(rows_of((BS, 256)) == place[:, at], 1.0, 0.0).astype(bf16)


def to_buses(values, block, selector):
    total = None
    pieces = [piece for v in values for piece in split3(v)]
    for j in range(block.shape[1] // CHUNK):
        at = slice(CHUNK * j, CHUNK * (j + 1))
        here = rows_of((PLANE, CHUNK)) == block[:, at]
        left = jnp.concatenate([jnp.where(here, p[:, at], 0.0).astype(bf16) for p in pieces], axis=0)
        part = contract_lanes(left, selector[:, at])
        total = part if total is None else total + part
    sums = [total[PLANE * k : PLANE * (k + 1)] for k in range(len(pieces))]
    return [sums[3 * q] + sums[3 * q + 1] + sums[3 * q + 2] for q in range(len(values))]


def to_lines(table, block, selector):
    left = jnp.concatenate([p.astype(bf16) for p in split3(table)], axis=0)
    picked = []
    for j in range(block.shape[1] // CHUNK):
        at = slice(CHUNK * j, CHUNK * (j + 1))
        found = jnp.dot(left, selector[:, at], preferred_element_type=f32)
        found = found[0:PLANE] + found[PLANE : 2 * PLANE] + found[2 * PLANE : 3 * PLANE]
        here = rows_of((PLANE, CHUNK)) == block[:, at]
        picked.append(jnp.sum(jnp.where(here, found, 0.0), axis=0, keepdims=True))
    half = len(picked) // 2
    return jnp.concatenate(picked[:half], axis=1) - jnp.concatenate(picked[half:], axis=1)


def endpoint_rows(ends, c, z):
    half = ends.shape[1] // 2
    at = pl.ds(pl.multiple_of(c * half, half), half)
    start, end = ends[0:1, at], ends[1:2, at]
    both = jnp.concatenate([start, end], axis=1)
    return start, end, both & (BS - 1), (both >> 8) - PLANE * z


def plane_peers(li, z, c):
    y, x = li // 4, lax.rem(li, 4)
    ys = [lax.rem(y + d, 4) for d in range(4)]
    xs = [lax.rem(x + d, 4) for d in range(4)]
    cs = [c, 1 - c]
    reach = [0, 1, 2, 1]
    offsets = [(dy, dx, dc) for dy in range(4) for dx in range(4) for dc in range(2)]
    offsets.sort(key=lambda o: -reach[o[0]] - reach[o[1]])
    peers = []
    for dy, dx, dc in offsets[:-2] + [(0, 0, 1)]:
        l2, c2 = ys[dy] * 4 + xs[dx], cs[dc]
        peers.append((c2 * 16 + l2, (l2, 2 * z + c2)))
    return peers


def depth_peers(li, z, c):
    return [(li, 2 * lax.rem(z + d, DEPTH) + c) for d in (4, 3, 5, 2, 6, 1, 7)]


def greet(li, z, c):
    barrier = pltpu.get_barrier_semaphore()
    for device in [device for _, device in plane_peers(li, z, c)] + depth_peers(li, z, c):
        pl.semaphore_signal(barrier, 1, device_id=device, device_id_type=MESH)


def greeted():
    pl.semaphore_wait(pltpu.get_barrier_semaphore(), PLANE - 1 + DEPTH - 1)


def send_plane(pick, home, slot, recv, sems, li, z, c):
    for place, device in plane_peers(li, z, c):
        pltpu.make_async_remote_copy(
            pick(place), recv.at[slot], sems.at[0], sems.at[1], device_id=device, device_id_type=MESH
        ).start()
    pltpu.make_async_copy(home, recv.at[slot], sems.at[1]).start()


def send_depth(src, recv, sems, li, z, c):
    for device in depth_peers(li, z, c):
        pltpu.make_async_remote_copy(
            src, recv.at[z], sems.at[0], sems.at[1], device_id=device, device_id_type=MESH
        ).start()
    pltpu.make_async_copy(src, recv.at[z], sems.at[1]).start()


def wait_bytes(ref, sem):
    pltpu.make_async_copy(ref, ref, sem).wait()


def sum_slots(recv, at):
    total = recv[0, :, at]
    for s in range(1, recv.shape[0]):
        total = total + recv[s, :, at]
    return total


def invert(work):
    n, w = work.shape[0], 32
    lane = lax.broadcasted_iota(jnp.int32, (w, 128), 1)
    row = rows_of((w, 128))
    lane1 = lax.broadcasted_iota(jnp.int32, (1, 128), 1)

    def panel(_, carry):
        ra, rb = work[0:w, 0:128], work[0:w, 128:256]
        for sub in range(w // 8):
            cols = [jnp.broadcast_to(ra[:, j : j + 1], (w, 128)) for j in range(8 * sub, 8 * sub + 8)]
            for k in range(8):
                r = 8 * sub + k
                ck = cols[k]
                rp = 1.0 / ck[r : r + 1, :]
                pa = jnp.where(lane1 == r, 1.0, ra[r : r + 1, :]) * rp
                pb = rb[r : r + 1, :] * rp
                here = row == r
                ra = jnp.where(here, pa, jnp.where(lane == r, 0.0, ra) - ck * pa)
                rb = jnp.where(here, pb, rb - ck * pb)
                for j in range(k + 1, 8):
                    cr = cols[j][r : r + 1, :] * rp
                    cols[j] = jnp.where(here, cr, cols[j] - ck * cr)
        top = jnp.concatenate([ra, rb], axis=1)
        rest = work[w:n, :]
        wide = jnp.concatenate([top, jnp.zeros((128 - w, n), f32)], axis=0)
        update = jnp.dot(rest[:, 0:128], wide, precision=lax.Precision.HIGHEST, preferred_element_type=f32)
        lanes = lax.broadcasted_iota(jnp.int32, (n - w, n), 1)
        rest = jnp.where(lanes < w, 0.0, rest) - update
        work[0 : n - w, :] = pltpu.roll(rest, n - w, 1)
        work[n - w : n, :] = pltpu.roll(top, n - w, 1)
        return carry

    lax.fori_loop(0, n // w, panel, 0)


def longest_step(now, step):
    return jnp.min(now / jnp.maximum(-step, now), axis=1, keepdims=True)


def buckets(owner, values, shift):
    order = jnp.where(rows_of((256, 256)) < lax.broadcasted_iota(jnp.int32, (256, 256), 1), 1.0, 0.0).astype(bf16)
    carry = jnp.zeros((PLANE, 1), f32)
    packed = None
    for j in range(owner.shape[1] // 256):
        at = slice(256 * j, 256 * (j + 1))
        here = rows_of((PLANE, 256)) == owner[:, at]
        marks = jnp.where(here, 1.0, 0.0)
        rank = jnp.dot(marks.astype(bf16), order, preferred_element_type=f32) + carry
        carry = carry + jnp.sum(marks, axis=1, keepdims=True)
        rank = jnp.sum(jnp.where(here, rank, 0.0), axis=0, keepdims=True)
        code = jnp.where(rank < SLOTS, rank + shift, -1.0)
        slots = jnp.where(rows_of((128, 256)).astype(f32) == code, 1.0, 0.0).astype(bf16)
        left = jnp.concatenate([jnp.where(here, v[:, at], 0.0).astype(bf16) for v in values], axis=0)
        piece = contract_lanes(left, slots)
        packed = piece if packed is None else packed + piece
    packed = [packed[PLANE * k : PLANE * (k + 1)] for k in range(len(values))]
    return packed, jnp.max(carry, axis=0, keepdims=True)


def bucket_lines(msg_in):
    group = 128 // SLOTS

    def candidates(g, at):
        return sum(msg_in[group * g + k, :, at] for k in range(1, group)) + msg_in[group * g, :, at]

    total = None
    near = rows_of((BS, 128)).astype(f32)
    for g in range(PLANE // group):
        p, q, d = (candidates(g, slice(512 + 128 * k, 640 + 128 * k)) for k in range(3))
        from_here, to_here = near == p, near == q
        right_side = jnp.concatenate(
            [jnp.where(to_here, 1.0, 0.0).astype(bf16), jnp.where(from_here, 1.0, 0.0).astype(bf16)], axis=1
        )
        for piece in split3(d):
            left = jnp.concatenate(
                [jnp.where(from_here, piece, 0.0).astype(bf16), jnp.where(to_here, piece, 0.0).astype(bf16)], axis=1
            )
            add = contract_lanes(left, right_side)
            total = add if total is None else total + add
    return total


def step_kernel(
    total_lines, given,
    primal, slacks, cost, ends, bus_dual, demand, normal,
    step_primal, step_slack, step_dual, lengths, fullest,
    selector, partner, msg, msg_in, diff0, diff0_in, part0, part0_in, block_in, work,
    solved, solved_in, diff, diff_in, part, part_in, solved2, solved2_in, diff2, diff2_in, final, final_in, last, last_in,
    fixed_sem, pair_sem, msg_sem, diff0_sem, part0_sem,
    solved_sem, diff_sem, part_sem, solved2_sem, diff2_sem, last_sem, final_sem,
):
    li, z, c = position()
    own = pltpu.make_async_copy(normal if given else normal.at[li], block_in, fixed_sem)
    own.start()
    greet(li, z, c)
    half = primal.shape[1] // 2
    mine = pl.ds(pl.multiple_of(c * half, half), half)
    at_home = c * 16 + li
    source = 2 * li + c
    lane1 = lax.broadcasted_iota(jnp.int32, (1, 128), 1)
    x, s = primal[:, mine], slacks[:, mine]
    start, end, place, block = endpoint_rows(ends, c, z)
    build_selector(selector, place)
    scaling = x / s
    inverse = 1.0 / s
    gap = jnp.sum(x * s, axis=1, keepdims=True)
    owner = jnp.where((start >> 8) == (end >> 8), block[:, :half], -1)
    shift = (SLOTS * lax.rem(source, 128 // SLOTS)).astype(f32)
    packed, most = buckets(
        owner, [place[:, :half].astype(f32), place[:, half:].astype(f32), *split3(scaling)], shift
    )
    ends_sum, third = to_buses(
        [jnp.concatenate([scaling, scaling], axis=1), jnp.concatenate([inverse, -inverse], axis=1)], block, selector
    )
    whole = jnp.concatenate(
        [ends_sum, third, packed[0], packed[1], packed[2] + packed[3] + packed[4], jnp.broadcast_to(gap, (PLANE, 128))],
        axis=1,
    )
    for b in range(PLANE):
        msg[b] = whole[b : b + 1]

    greeted()
    pair = pltpu.make_async_remote_copy(
        bus_dual, partner, pair_sem.at[0], pair_sem.at[1], device_id=(li, 2 * z + 1 - c), device_id_type=MESH
    )
    pair.start()
    send_plane(lambda b: msg.at[b], msg.at[at_home], source, msg_in, msg_sem, li, z, c)

    pair.wait()
    mine_dual = jnp.concatenate([bus_dual[:, BS * k : BS * (k + 1)] for k in range(16)], axis=0)
    other_dual = jnp.concatenate([partner[:, BS * k : BS * (k + 1)] for k in range(16)], axis=0)
    table = jnp.concatenate(
        [jnp.where(c == 0, mine_dual, other_dual), jnp.where(c == 0, other_dual, mine_dual)], axis=0
    )
    diff0[:, :half] = to_lines(table, block, selector)
    diff0[:, half:] = jnp.broadcast_to(most, (1, 128))
    send_depth(diff0, diff0_in, diff0_sem, li, z, c)

    wait_bytes(msg_in, msg_sem.at[1])
    sums = sum_slots(msg_in, slice(0, 512))
    third = sums[:, 256:]
    gap0 = sum_slots(msg_in, slice(896, 1024))[:, 0:1]
    own.wait()
    if given:
        work[...] = block_in[...]
    else:
        diagonal = rows_of((BS, BS)) == lax.broadcasted_iota(jnp.int32, (BS, BS), 1)
        work[...] = block_in[...] + jnp.where(diagonal, sums[:, :256], 0.0) - bucket_lines(msg_in)

    wait_bytes(diff0_in, diff0_sem.at[1])
    dual_res = cost[:, mine] - sum_slots(diff0_in, slice(0, half)) - s
    most = diff0_in[0, :, half:]
    for k in range(1, DEPTH):
        most = jnp.maximum(most, diff0_in[k, :, half:])
    flow = scaling * dual_res
    (right,) = to_buses([jnp.concatenate([flow, -flow], axis=1)], block, selector)
    whole = jnp.concatenate([right, jnp.broadcast_to(most, (PLANE, 128))], axis=1)
    for b in range(PLANE):
        part0[b] = whole[b : b + 1]
    send_plane(lambda b: part0.at[b], part0.at[at_home], source, part0_in, part0_sem, li, z, c)
    invert(work)
    wait_bytes(part0_in, part0_sem.at[1])
    right = demand[:, pl.ds(pl.multiple_of(li * BS, BS), BS)] + sum_slots(part0_in, slice(0, 256))
    most = part0_in[0, :, 256:]
    for k in range(1, PLANE):
        most = jnp.maximum(most, part0_in[k, :, 256:])
    fullest[...] = most[:, 0:1]

    def solve(vector):
        wide = jnp.broadcast_to(vector, (8, BS))
        return jnp.dot(wide, work[...], precision=lax.Precision.HIGHEST, preferred_element_type=f32)[0:1]

    solved[...] = solve(right)
    send_plane(lambda b: solved, solved, at_home, solved_in, solved_sem, li, z, c)
    wait_bytes(solved_in, solved_sem.at[1])
    table = jnp.concatenate([solved_in[b] for b in range(PLANE)], axis=0)
    diff[...] = to_lines(table, block, selector)
    send_depth(diff, diff_in, diff_sem, li, z, c)
    wait_bytes(diff_in, diff_sem.at[1])
    affine_slack = dual_res - sum_slots(diff_in, slice(0, half))
    affine_primal = -x - scaling * affine_slack
    cross = affine_primal * affine_slack
    extra = cross / s
    (sums,) = to_buses([jnp.concatenate([extra, -extra], axis=1)], block, selector)
    scalars = [
        longest_step(x, affine_primal),
        longest_step(s, affine_slack),
        jnp.sum(affine_primal * s, axis=1, keepdims=True),
        jnp.sum(x * affine_slack, axis=1, keepdims=True),
        jnp.sum(cross, axis=1, keepdims=True),
    ]
    row = jnp.zeros((1, 128), f32)
    for k, value in enumerate(scalars):
        row = jnp.where(lane1 == k, value, row)
    whole = jnp.concatenate([sums, jnp.broadcast_to(row, (PLANE, 128))], axis=1)
    for b in range(PLANE):
        part[b] = whole[b : b + 1]
    send_plane(lambda b: part.at[b], part.at[at_home], source, part_in, part_sem, li, z, c)
    wait_bytes(part_in, part_sem.at[1])

    added = sum_slots(part_in, slice(0, 384))
    least = part_in[0, :, 256:384]
    for k in range(1, PLANE):
        least = jnp.minimum(least, part_in[k, :, 256:384])
    take_p, take_d = least[:, 0:1], least[:, 1:2]
    tail = added[:, 256:384]
    gap_affine = gap0 + take_p * tail[:, 2:3] + take_d * tail[:, 3:4] + take_p * take_d * tail[:, 4:5]
    ratio = gap_affine / gap0
    aim = ratio * ratio * ratio * (gap0 / total_lines)
    solved2[...] = solve(right - aim * third + added[:, :256])
    send_plane(lambda b: solved2, solved2, at_home, solved2_in, solved2_sem, li, z, c)
    wait_bytes(solved2_in, solved2_sem.at[1])
    table = jnp.concatenate([solved2_in[b] for b in range(PLANE)], axis=0)
    diff2[...] = to_lines(table, block, selector)
    send_depth(diff2, diff2_in, diff2_sem, li, z, c)
    for b in range(16):
        step_dual[:, BS * b : BS * (b + 1)] = solved2_in[16 * c + b]
    wait_bytes(diff2_in, diff2_sem.at[1])
    slack = dual_res - sum_slots(diff2_in, slice(0, half))
    primal_step = (aim - x * s - cross) / s - scaling * slack
    last[...] = jnp.where(lane1 == 0, longest_step(x, primal_step), longest_step(s, slack))
    final[0:1] = primal_step
    final[1:2] = slack
    send_plane(lambda b: last, last, source, last_in, last_sem, li, z, c)
    pair2 = pltpu.make_async_remote_copy(
        final, final_in, final_sem.at[0], final_sem.at[1], device_id=(li, 2 * z + 1 - c), device_id_type=MESH
    )
    pair2.start()
    step_primal[:, mine] = primal_step
    step_slack[:, mine] = slack
    pair2.wait()
    other = pl.ds(pl.multiple_of((1 - c) * half, half), half)
    step_primal[:, other] = final_in[0:1]
    step_slack[:, other] = final_in[1:2]
    for recv, sems in (
        (msg_in, msg_sem), (diff0_in, diff0_sem), (part0_in, part0_sem), (solved_in, solved_sem), (diff_in, diff_sem),
        (part_in, part_sem), (solved2_in, solved2_sem), (diff2_in, diff2_sem), (last_in, last_sem),
    ):
        wait_bytes(recv.at[pl.ds(0, recv.shape[0] - 1)], sems.at[0])
    wait_bytes(last_in, last_sem.at[1])
    least = last_in[0]
    for k in range(1, PLANE):
        least = jnp.minimum(least, last_in[k])
    lengths[...] = damping * least


def vmem(n):
    return [pl.BlockSpec(memory_space=pltpu.VMEM)] * n


def struct(*shape):
    return jax.ShapeDtypeStruct(shape, f32)


def scattered_block(primal, slacks, endpoints, fixed_part):
    blocks_here, block_size = fixed_part.shape[0], fixed_part.shape[1]
    buses_here = blocks_here * block_size
    scaling = primal / slacks
    local = endpoints - lax.axis_index("bus") * buses_here
    own_from, own_to = jnp.where((local >= 0) & (local < buses_here), local, buses_here)
    same_block = endpoints[0] // block_size == endpoints[1] // block_size
    crossing = jnp.where(same_block, -scaling, jnp.zeros_like(scaling))
    rows = jnp.concatenate([own_from, own_to, own_from, own_to])
    columns = jnp.concatenate([own_from, own_to, own_to, own_from]) % block_size
    values = jnp.concatenate([scaling, scaling, crossing, crossing])
    flat = jnp.zeros((buses_here * block_size,), f32).at[rows * block_size + columns].add(values, mode="drop")
    tiles = lax.all_to_all(flat.reshape(blocks_here, block_size, block_size), "line", 0, 0, tiled=True)
    mine = lax.dynamic_index_in_dim(fixed_part, lax.axis_index("line"), 0, keepdims=False)
    return mine + jnp.sum(tiles, axis=0)


def hand_over(step_primal, step_slack, step_dual, lengths, primal_out, slack_out, dual_out, lengths_out):
    primal_out[...] = step_primal[...]
    slack_out[...] = step_slack[...]
    dual_out[...] = step_dual[...]
    lengths_out[...] = lengths[:, 0:2]


def whole_step(given, args, normal):
    x, s, cost, ends, bus_dual, demand = args
    lines_here, buses_here = x.shape[1], bus_dual.shape[1]
    half = lines_here // 2
    total_lines = float(lines_here * lax.axis_size("line"))
    dma = pltpu.SemaphoreType.DMA
    exchange = lambda slots, width: [pltpu.VMEM((1, width), f32), pltpu.VMEM((slots, 1, width), f32)]
    buckets_of = lambda width: [pltpu.VMEM((PLANE, 1, width), f32)] * 2
    return pl.pallas_call(
        functools.partial(step_kernel, total_lines, given),
        out_shape=(struct(1, lines_here), struct(1, lines_here), struct(1, buses_here), struct(1, 128), struct(1, 1)),
        in_specs=vmem(6) + [pl.BlockSpec(memory_space=pl.ANY)],
        out_specs=tuple(vmem(5)),
        scratch_shapes=[pltpu.VMEM((BS, lines_here), bf16), pltpu.VMEM((1, buses_here), f32)]
        + buckets_of(1024)
        + exchange(DEPTH, half + 128)
        + buckets_of(384)
        + [pltpu.VMEM((BS, BS), f32)] * 2
        + exchange(PLANE, BS)
        + exchange(DEPTH, half)
        + buckets_of(384)
        + exchange(PLANE, BS)
        + exchange(DEPTH, half)
        + [pltpu.VMEM((2, half), f32)] * 2
        + exchange(PLANE, 128)
        + [dma]
        + [dma((2,))] * 11,
        compiler_params=pltpu.CompilerParams(collective_id=int(given), has_side_effects=True),
        name="step_given" if given else "step",
    )(*args, normal)


def per_device(primal, slacks, line_cost, bus_dual, demand, endpoints, fixed_part):
    args = tuple(a.reshape(1, -1) for a in (primal, slacks, line_cost))
    args += (endpoints, bus_dual.reshape(1, -1), demand.reshape(1, -1))
    *steps, fullest = whole_step(False, args, fixed_part)

    def out(step_primal, step_slack, step_dual, lengths):
        return pl.pallas_call(
            hand_over,
            out_shape=tuple(struct(*a.shape) for a in (step_primal, step_slack, step_dual)) + (struct(1, 2),),
            in_specs=vmem(4),
            out_specs=tuple(vmem(4)),
            name="hand_over",
        )(step_primal, step_slack, step_dual, lengths)

    def again():
        normal = scattered_block(primal, slacks, endpoints, fixed_part)
        return out(*whole_step(True, args, normal)[:4])

    outputs = lax.cond(fullest[0, 0] > SLOTS, again, lambda: out(*steps))
    return tuple(a.reshape(-1) for a in outputs)


def solution(mesh):
    in_specs = (P("line"), P("line"), P("line"), P("bus"), P("bus"), P(None, "line"), P("bus", None, None))
    out_specs = (P("line"), P("line"), P("bus"), P())
    return jax.shard_map(per_device, mesh=mesh, in_specs=in_specs, out_specs=out_specs, check_vma=False)
```

time: 76.2 us -> 65.4 us (0.86)
  Pallas kernels: 73.4 us -> 60.1 us
  local copies, waits for them, and re-layouts: 1.21 us -> 3.38 us
    pallas_call x4 -> x2, Pallas kernels: 73.4 us -> 60.1 us  [the longest x1 59.5 us: whole_step(): pl.pallas_call(functools.partial(step_kernel, total_lines, given), out_sh...]
    cond x0 -> x4, local copies, waits for them, and re-layouts: none -> 2.75 us
    slice x1 -> x0, local copies, waits for them, and re-layouts: 1.19 us -> none  [per_device(): scal[1, 0] > SLOTS]
where the time goes in v3:
time: 65.4 us; the launch traced here: 64.9 us
  Pallas kernels  60.1 us (92%)
  local copies, waits for them, and re-layouts  3.38 us (5%)
  between operations  1.39 us (2%)
    pallas_call x1, Pallas kernels, whole_step(): pl.pallas_call(functools.partial(step_kernel, total_lines, given), out_sh...  59.5 us
    cond x4, local copies, waits for them, and re-layouts  2.75 us

profile of v3, /device:TPU:1, one launch (start us, length us, event | category | flops | bytes accessed | tf_op | source)
XLA Modules:
  0.0 64.9 jit_solution(7339312290227279696)
XLA Ops:
  0.6 0.0 copy-start
  0.6 0.0 copy-start.2
  0.7 0.0 copy-start.1
  0.7 0.0 copy-start.4
  0.7 0.0 copy-start.3
  0.7 0.0 copy-start.5
  0.7 59.5 %step.1 = (f32[1,3072]{1,0:T(1,128)S(1)}, f32[1,3072]{1,0:T(1,128)S(1)}, f32[1,4096]{1,0:T(1,128)S(1)}, f32[1,128]{1,0:T(1,128)S(1)}, f32[1,1]{1,0:T(1,128)}) custom-call(f32[1,3072]{1,0:T(1,128)} %bitcast.19, f32[1,3072]{1,0:T(1,128)} %bitcast.22, f32[1,3072]{1,0:T(1,128)} %bitcast.29, s32[2,3072]{1,0:T(2,128)} %ends.1, f32[1,4096]{1,0:T(1,128)} %bitcast.25, ...), custom_call_target="tpu_custom_call" | custom-call | tf_op jit(solution)/shard_map/step/pallas_call | solution.py:428
  60.8 0.0 copy-done
  60.9 0.0 copy-done.2
  60.9 0.0 copy-done.1
  60.9 0.0 copy-done.4
  60.9 0.0 copy-done.3
  60.9 0.0 copy-done.5
  60.9 3.4 %conditional.1 = ((f32[1,3072]{1,0:T(1,128)}, f32[1,3072]{1,0:T(1,128)}, f32[1,4096]{1,0:T(1,128)}, f32[1,2]{1,0:T(1,128)}), (f32[1,3072]{1,0:T(1,128)S(1)}, f32...) conditional(s32[]{:T(128)} %bitcast.11, (f32[1,3072]{1,0:T(1,128)S(1)}, f32[1,3072]{1,0:T(1,128)S(1)}, ...), branch_computations={%region_0.0_spmd, %region_1.4_spmd} | conditional | flops 1490953 | bytes 30859472 | solution.py:470
  60.9 0.6 hand_over.2
  61.5 0.7 %copy.35 = f32[1,3072]{1,0:T(1,128)S(1)} copy(f32[1,3072]{1,0:T(1,128)} %get-tuple-element.135) | data formatting | bytes 24576 | tf_op jit(solution)/shard_map/cond
  62.2 0.7 %copy.36 = f32[1,3072]{1,0:T(1,128)S(1)} copy(f32[1,3072]{1,0:T(1,128)} %get-tuple-element.136) | data formatting | bytes 24576 | tf_op jit(solution)/shard_map/cond
  63.0 0.7 %copy.37 = f32[1,4096]{1,0:T(1,128)S(1)} copy(f32[1,4096]{1,0:T(1,128)} %get-tuple-element.137) | data formatting | bytes 32768 | tf_op jit(solution)/shard_map/cond
  63.7 0.6 copy.38
  64.3 0.0 copy-start.6
  64.3 0.0 copy-start.7
  64.3 0.0 copy-start.8
  64.3 0.0 copy-start.9
  64.3 0.6 copy-done.6
  64.9 0.0 copy-done.7
  64.9 0.0 copy-done.8
  64.9 0.0 copy-done.9
Async XLA Ops:
  0.6 60.2 %copy-start = (s32[2,3072]{1,0:T(2,128)S(1)}, s32[2,3072]{1,0:T(2,128)}, u32[]{:S(2)}) copy-start(s32[2,3072]{1,0:T(2,128)} %ends.1) | copy-start | bytes 73732
  0.6 60.2 %copy-start.2 = (f32[3072]{0:T(1024)S(1)}, f32[3072]{0:T(1024)}, u32[]{:S(2)}) copy-start(f32[3072]{0:T(1024)} %param.10) | copy-start | bytes 36868
  0.7 60.2 %copy-start.1 = (f32[3072]{0:T(1024)S(1)}, f32[3072]{0:T(1024)}, u32[]{:S(2)}) copy-start(f32[3072]{0:T(1024)} %param.9) | copy-start | bytes 36868
  0.7 60.2 %copy-start.4 = (f32[4096]{0:T(1024)S(1)}, f32[4096]{0:T(1024)}, u32[]{:S(2)}) copy-start(f32[4096]{0:T(1024)} %param.13) | copy-start | bytes 49156
  0.7 60.2 %copy-start.3 = (f32[4096]{0:T(1024)S(1)}, f32[4096]{0:T(1024)}, u32[]{:S(2)}) copy-start(f32[4096]{0:T(1024)} %param.12) | copy-start | bytes 49156
  0.7 60.2 %copy-start.5 = (f32[3072]{0:T(1024)S(1)}, f32[3072]{0:T(1024)}, u32[]{:S(2)}) copy-start(f32[3072]{0:T(1024)} %param.11) | copy-start | bytes 36868
  64.3 0.6 copy-start.6
  64.3 0.6 copy-start.7
  64.3 0.6 copy-start.8
  64.3 0.6 copy-start.9

commit v4 on v3

--- a/solution.py
+++ b/solution.py
@@ -75,10 +75,8 @@
     return jnp.concatenate(picked[:half], axis=1) - jnp.concatenate(picked[half:], axis=1)
 
 
-def endpoint_rows(ends, c, z):
-    half = ends.shape[1] // 2
-    at = pl.ds(pl.multiple_of(c * half, half), half)
-    start, end = ends[0:1, at], ends[1:2, at]
+def endpoint_rows(ends, z):
+    start, end = ends[0:1, :], ends[1:2, :]
     both = jnp.concatenate([start, end], axis=1)
     return start, end, both & (BS - 1), (both >> 8) - PLANE * z
 
@@ -139,39 +137,70 @@
     return total
 
 
-def invert(work):
+def eliminate(pa, pb, off):
+    groups = len(pa)
+    lane, row = lax.broadcasted_iota(jnp.int32, (8, 128), 1), rows_of((8, 128))
+
+    def spread(sub):
+        first = off + 8 * sub
+        return [[jnp.broadcast_to(p[:, j : j + 1], (8, 128)) for p in pa] for j in range(first, first + 8)]
+
+    columns, ahead = spread(0), None
+    for sub in range(groups):
+        first = off + 8 * sub
+        inside = (lane >= first) & (lane < first + 8)
+        unit = jnp.where(lane - first == row, 1.0, 0.0)
+        pa = [jnp.where(inside, unit if g == sub else 0.0, pa[g]) for g in range(groups)]
+        for k in range(8):
+            if k == 3 and sub + 1 < groups:
+                ahead = spread(sub + 1)
+            pivot = columns[k]
+            scale = 1.0 / pivot[sub][k : k + 1]
+            here = row == k
+
+            def swept(rows):
+                top = rows[sub][k : k + 1] * scale
+                rest = [rows[g] - pivot[g] * top for g in range(groups)]
+                rest[sub] = jnp.where(here, top, rest[sub])
+                return rest
+
+            columns = columns[: k + 1] + [swept(c) for c in columns[k + 1 :]]
+            if ahead is not None:
+                ahead = [swept(c) for c in ahead]
+            pa, pb = swept(pa), swept(pb)
+        columns, ahead = ahead, None
+    return pa, pb
+
+
+def invert(work, between):
     n, w = work.shape[0], 32
-    lane = lax.broadcasted_iota(jnp.int32, (w, 128), 1)
-    row = rows_of((w, 128))
-    lane1 = lax.broadcasted_iota(jnp.int32, (1, 128), 1)
-
-    def panel(_, carry):
-        ra, rb = work[0:w, 0:128], work[0:w, 128:256]
-        for sub in range(w // 8):
-            cols = [jnp.broadcast_to(ra[:, j : j + 1], (w, 128)) for j in range(8 * sub, 8 * sub + 8)]
-            for k in range(8):
-                r = 8 * sub + k
-                ck = cols[k]
-                rp = 1.0 / ck[r : r + 1, :]
-                pa = jnp.where(lane1 == r, 1.0, ra[r : r + 1, :]) * rp
-                pb = rb[r : r + 1, :] * rp
-                here = row == r
-                ra = jnp.where(here, pa, jnp.where(lane == r, 0.0, ra) - ck * pa)
-                rb = jnp.where(here, pb, rb - ck * pb)
-                for j in range(k + 1, 8):
-                    cr = cols[j][r : r + 1, :] * rp
-                    cols[j] = jnp.where(here, cr, cols[j] - ck * cr)
-        top = jnp.concatenate([ra, rb], axis=1)
-        rest = work[w:n, :]
-        wide = jnp.concatenate([top, jnp.zeros((128 - w, n), f32)], axis=0)
-        update = jnp.dot(rest[:, 0:128], wide, precision=lax.Precision.HIGHEST, preferred_element_type=f32)
-        lanes = lax.broadcasted_iota(jnp.int32, (n - w, n), 1)
-        rest = jnp.where(lanes < w, 0.0, rest) - update
-        work[0 : n - w, :] = pltpu.roll(rest, n - w, 1)
-        work[n - w : n, :] = pltpu.roll(top, n - w, 1)
-        return carry
-
-    lax.fori_loop(0, n // w, panel, 0)
+    now = work[0:w, :]
+    for i in range(n // w):
+        slab, off = divmod(w * i, 128)
+        a = slice(128 * slab, 128 * slab + 128)
+        b = slice(128 - 128 * slab, 256 - 128 * slab)
+        groups = range(0, w, 8)
+        pa, pb = eliminate([now[g : g + 8, a] for g in groups], [now[g : g + 8, b] for g in groups], off)
+        pa, pb = jnp.concatenate(pa, axis=0), jnp.concatenate(pb, axis=0)
+        top = jnp.concatenate([pa, pb] if slab == 0 else [pb, pa], axis=1)
+        parts = [jnp.zeros((off, n), f32)] * (off > 0) + [top]
+        parts += [jnp.zeros((128 - w - off, n), f32)] * (off + w < 128)
+        wide = jnp.concatenate(parts, axis=0)
+
+        def take(rows):
+            lanes = lax.broadcasted_iota(jnp.int32, rows.shape, 1)
+            kept = jnp.where((lanes >= w * i) & (lanes < w * i + w), 0.0, rows)
+            return kept - jnp.dot(rows[:, a], wide, precision=lax.Precision.HIGHEST, preferred_element_type=f32)
+
+        low, high = w * i, w * i + w
+        work[low:high, :] = top
+        if high < n:
+            now = take(work[high : high + w, :])
+        if high + w < n:
+            work[high + w : n, :] = take(work[high + w : n, :])
+        if low > 0:
+            work[0:low, :] = take(work[0:low, :])
+        between(i)
 
 
 def longest_step(now, step):
@@ -207,7 +236,7 @@
     total = None
     near = rows_of((BS, 128)).astype(f32)
     for g in range(PLANE // group):
-        p, q, d = (candidates(g, slice(512 + 128 * k, 640 + 128 * k)) for k in range(3))
+        p, q, d = (candidates(g, slice(256 + 128 * k, 384 + 128 * k)) for k in range(3))
         from_here, to_here = near == p, near == q
         right_side = jnp.concatenate(
             [jnp.where(to_here, 1.0, 0.0).astype(bf16), jnp.where(from_here, 1.0, 0.0).astype(bf16)], axis=1
@@ -223,25 +252,44 @@
 
 def step_kernel(
     total_lines, given,
-    primal, slacks, cost, ends, bus_dual, demand, normal,
+    primal_all, slacks_all, cost_all, ends_all, bus_dual_all, demand_all, normal,
     step_primal, step_slack, step_dual, lengths, fullest,
-    selector, partner, msg, msg_in, diff0, diff0_in, part0, part0_in, block_in, work,
+    primal, slacks, cost, ends, bus_dual, demand, selector, partner, msg, msg_in, diff0, diff0_in, part0, part0_in, block_in, work, dual_res,
     solved, solved_in, diff, diff_in, part, part_in, solved2, solved2_in, diff2, diff2_in, final, final_in, last, last_in,
-    fixed_sem, pair_sem, msg_sem, diff0_sem, part0_sem,
+    in_sem, fixed_sem, pair_sem, msg_sem, diff0_sem, part0_sem,
     solved_sem, diff_sem, part_sem, solved2_sem, diff2_sem, last_sem, final_sem,
 ):
     li, z, c = position()
+    greet(li, z, c)
+    half = primal.shape[1]
+    mine = pl.ds(pl.multiple_of(c * half, half), half)
+    own_buses = pl.ds(pl.multiple_of(li * BS, BS), BS)
+    copies = [
+        pltpu.make_async_copy(src, dst, in_sem.at[k])
+        for k, (src, dst) in enumerate(
+            (
+                (ends_all.at[:, mine], ends),
+                (primal_all.at[:, mine], primal),
+                (slacks_all.at[:, mine], slacks),
+                (bus_dual_all, bus_dual),
+                (cost_all.at[:, mine], cost),
+                (demand_all.at[:, own_buses], demand),
+            )
+        )
+    ]
+    for copy in copies:
+        copy.start()
     own = pltpu.make_async_copy(normal if given else normal.at[li], block_in, fixed_sem)
     own.start()
-    greet(li, z, c)
-    half = primal.shape[1] // 2
-    mine = pl.ds(pl.multiple_of(c * half, half), half)
     at_home = c * 16 + li
     source = 2 * li + c
     lane1 = lax.broadcasted_iota(jnp.int32, (1, 128), 1)
-    x, s = primal[:, mine], slacks[:, mine]
-    start, end, place, block = endpoint_rows(ends, c, z)
+    copies[0].wait()
+    start, end, place, block = endpoint_rows(ends, z)
     build_selector(selector, place)
+    copies[1].wait()
+    copies[2].wait()
+    x, s = primal[...], slacks[...]
     scaling = x / s
     inverse = 1.0 / s
     gap = jnp.sum(x * s, axis=1, keepdims=True)
@@ -250,15 +298,15 @@
     packed, most = buckets(
         owner, [place[:, :half].astype(f32), place[:, half:].astype(f32), *split3(scaling)], shift
     )
-    ends_sum, third = to_buses(
-        [jnp.concatenate([scaling, scaling], axis=1), jnp.concatenate([inverse, -inverse], axis=1)], block, selector
-    )
+    (ends_sum,) = to_buses([jnp.concatenate([scaling, scaling], axis=1)], block, selector)
     whole = jnp.concatenate(
-        [ends_sum, third, packed[0], packed[1], packed[2] + packed[3] + packed[4], jnp.broadcast_to(gap, (PLANE, 128))],
+        [ends_sum, packed[0], packed[1], packed[2] + packed[3] + packed[4], jnp.broadcast_to(gap, (PLANE, 128))],
         axis=1,
     )
     for b in range(PLANE):
         msg[b] = whole[b : b + 1]
+    for copy in copies[3:]:
+        copy.wait()
 
     greeted()
     pair = pltpu.make_async_remote_copy(
@@ -278,34 +326,37 @@
     send_depth(diff0, diff0_in, diff0_sem, li, z, c)
 
     wait_bytes(msg_in, msg_sem.at[1])
-    sums = sum_slots(msg_in, slice(0, 512))
-    third = sums[:, 256:]
-    gap0 = sum_slots(msg_in, slice(896, 1024))[:, 0:1]
+    sums = sum_slots(msg_in, slice(0, 256))
+    gap0 = sum_slots(msg_in, slice(640, 768))[:, 0:1]
     own.wait()
     if given:
         work[...] = block_in[...]
     else:
         diagonal = rows_of((BS, BS)) == lax.broadcasted_iota(jnp.int32, (BS, BS), 1)
-        work[...] = block_in[...] + jnp.where(diagonal, sums[:, :256], 0.0) - bucket_lines(msg_in)
-
-    wait_bytes(diff0_in, diff0_sem.at[1])
-    dual_res = cost[:, mine] - sum_slots(diff0_in, slice(0, half)) - s
-    most = diff0_in[0, :, half:]
-    for k in range(1, DEPTH):
-        most = jnp.maximum(most, diff0_in[k, :, half:])
-    flow = scaling * dual_res
-    (right,) = to_buses([jnp.concatenate([flow, -flow], axis=1)], block, selector)
-    whole = jnp.concatenate([right, jnp.broadcast_to(most, (PLANE, 128))], axis=1)
-    for b in range(PLANE):
-        part0[b] = whole[b : b + 1]
-    send_plane(lambda b: part0.at[b], part0.at[at_home], source, part0_in, part0_sem, li, z, c)
-    invert(work)
+        work[...] = block_in[...] + jnp.where(diagonal, sums, 0.0) - bucket_lines(msg_in)
+
+    def first_right_side(panel):
+        if panel != 1:
+            return
+        wait_bytes(diff0_in, diff0_sem.at[1])
+        residual = cost[...] - sum_slots(diff0_in, slice(0, half)) - s
+        dual_res[...] = residual
+        most = diff0_in[0, :, half:]
+        for k in range(1, DEPTH):
+            most = jnp.maximum(most, diff0_in[k, :, half:])
+        flow = scaling * residual
+        sums = to_buses(
+            [jnp.concatenate([flow, -flow], axis=1), jnp.concatenate([inverse, -inverse], axis=1)], block, selector
+        )
+        whole = jnp.concatenate([*sums, jnp.broadcast_to(most, (PLANE, 128))], axis=1)
+        for b in range(PLANE):
+            part0[b] = whole[b : b + 1]
+        send_plane(lambda b: part0.at[b], part0.at[at_home], source, part0_in, part0_sem, li, z, c)
+
+    invert(work, first_right_side)
     wait_bytes(part0_in, part0_sem.at[1])
-    right = demand[:, pl.ds(pl.multiple_of(li * BS, BS), BS)] + sum_slots(part0_in, slice(0, 256))
-    most = part0_in[0, :, 256:]
-    for k in range(1, PLANE):
-        most = jnp.maximum(most, part0_in[k, :, 256:])
-    fullest[...] = most[:, 0:1]
+    sums = sum_slots(part0_in, slice(0, 512))
+    right, third = demand[...] + sums[:, :256], sums[:, 256:]
 
     def solve(vector):
         wide = jnp.broadcast_to(vector, (8, BS))
@@ -318,7 +369,7 @@
     diff[...] = to_lines(table, block, selector)
     send_depth(diff, diff_in, diff_sem, li, z, c)
     wait_bytes(diff_in, diff_sem.at[1])
-    affine_slack = dual_res - sum_slots(diff_in, slice(0, half))
+    affine_slack = dual_res[...] - sum_slots(diff_in, slice(0, half))
     affine_primal = -x - scaling * affine_slack
     cross = affine_primal * affine_slack
     extra = cross / s
@@ -357,7 +408,7 @@
     for b in range(16):
         step_dual[:, BS * b : BS * (b + 1)] = solved2_in[16 * c + b]
     wait_bytes(diff2_in, diff2_sem.at[1])
-    slack = dual_res - sum_slots(diff2_in, slice(0, half))
+    slack = dual_res[...] - sum_slots(diff2_in, slice(0, half))
     primal_step = (aim - x * s - cross) / s - scaling * slack
     last[...] = jnp.where(lane1 == 0, longest_step(x, primal_step), longest_step(s, slack))
     final[0:1] = primal_step
@@ -369,6 +420,10 @@
     pair2.start()
     step_primal[:, mine] = primal_step
     step_slack[:, mine] = slack
+    most = part0_in[0, :, 512:]
+    for k in range(1, PLANE):
+        most = jnp.maximum(most, part0_in[k, :, 512:])
+    fullest[...] = most[:, 0:1]
     pair2.wait()
     other = pl.ds(pl.multiple_of((1 - c) * half, half), half)
     step_primal[:, other] = final_in[0:1]
@@ -428,13 +483,16 @@
     return pl.pallas_call(
         functools.partial(step_kernel, total_lines, given),
         out_shape=(struct(1, lines_here), struct(1, lines_here), struct(1, buses_here), struct(1, 128), struct(1, 1)),
-        in_specs=vmem(6) + [pl.BlockSpec(memory_space=pl.ANY)],
+        in_specs=[pl.BlockSpec(memory_space=pl.ANY)] * 7,
         out_specs=tuple(vmem(5)),
-        scratch_shapes=[pltpu.VMEM((BS, lines_here), bf16), pltpu.VMEM((1, buses_here), f32)]
-        + buckets_of(1024)
+        scratch_shapes=[pltpu.VMEM((1, half), f32)] * 3
+        + [pltpu.VMEM((2, half), jnp.int32), pltpu.VMEM((1, buses_here), f32), pltpu.VMEM((1, BS), f32)]
+        + [pltpu.VMEM((BS, lines_here), bf16), pltpu.VMEM((1, buses_here), f32)]
+        + buckets_of(768)
         + exchange(DEPTH, half + 128)
-        + buckets_of(384)
+        + buckets_of(640)
         + [pltpu.VMEM((BS, BS), f32)] * 2
+        + [pltpu.VMEM((1, half), f32)]
         + exchange(PLANE, BS)
         + exchange(DEPTH, half)
         + buckets_of(384)
@@ -442,7 +500,7 @@
         + exchange(DEPTH, half)
         + [pltpu.VMEM((2, half), f32)] * 2
         + exchange(PLANE, 128)
-        + [dma]
+        + [dma((6,)), dma]
         + [dma((2,))] * 11,
         compiler_params=pltpu.CompilerParams(collective_id=int(given), has_side_effects=True),
         name="step_given" if given else "step",
@@ -452,22 +510,19 @@
 def per_device(primal, slacks, line_cost, bus_dual, demand, endpoints, fixed_part):
     args = tuple(a.reshape(1, -1) for a in (primal, slacks, line_cost))
     args += (endpoints, bus_dual.reshape(1, -1), demand.reshape(1, -1))
-    *steps, fullest = whole_step(False, args, fixed_part)
-
-    def out(step_primal, step_slack, step_dual, lengths):
-        return pl.pallas_call(
-            hand_over,
-            out_shape=tuple(struct(*a.shape) for a in (step_primal, step_slack, step_dual)) + (struct(1, 2),),
-            in_specs=vmem(4),
-            out_specs=tuple(vmem(4)),
-            name="hand_over",
-        )(step_primal, step_slack, step_dual, lengths)
-
-    def again():
+    def again(steps):
         normal = scattered_block(primal, slacks, endpoints, fixed_part)
-        return out(*whole_step(True, args, normal)[:4])
-
-    outputs = lax.cond(fullest[0, 0] > SLOTS, again, lambda: out(*steps))
+        *steps, fullest = whole_step(True, args, normal)
+        return (*steps, jnp.zeros_like(fullest))
+
+    *steps, _ = lax.while_loop(lambda steps: steps[-1][0, 0] > SLOTS, again, tuple(whole_step(False, args, fixed_part)))
+    outputs = pl.pallas_call(
+        hand_over,
+        out_shape=tuple(struct(*a.shape) for a in steps[:3]) + (struct(1, 2),),
+        in_specs=vmem(4),
+        out_specs=tuple(vmem(4)),
+        name="hand_over",
+    )(*steps)
     return tuple(a.reshape(-1) for a in outputs)
 
 

time: 65.4 us -> 60.6 us (0.927)
  local copies, waits for them, and re-layouts: 3.38 us -> 0.03 us
  Pallas kernels: 60.1 us -> 58.7 us
  loops' own time: 0.01 us -> 0.91 us
    cond x4 -> x0, local copies, waits for them, and re-layouts: 2.75 us -> none
    pallas_call x1, Pallas kernels: 59.5 us -> 57.3 us  [whole_step(): pl.pallas_call(functools.partial(step_kernel, total_lines, given), out_sh...]
    another operation x1, loops' own time: 0.01 us -> 0.91 us  [per_device(): lax.while_loop(lambda steps: steps[-1][0, 0] > SLOTS, again, tuple(whole_...]
    pallas_call x1, Pallas kernels: 0.62 us -> 1.37 us  [per_device(): pl.pallas_call(hand_over, out_shape=tuple((struct(*a.shape) for a in step...]
where the time goes in v4:
time: 60.6 us; the launch traced here: 60.4 us
  Pallas kernels  58.7 us (97%)
  loops' own time  0.91 us (2%)
  between operations  0.74 us (1%)
    pallas_call x1, Pallas kernels, whole_step(): pl.pallas_call(functools.partial(step_kernel, total_lines, given), out_sh...  57.3 us
    pallas_call x1, Pallas kernels, per_device(): pl.pallas_call(hand_over, out_shape=tuple((struct(*a.shape) for a in step...  1.37 us

profile of v4, /device:TPU:1, one launch (start us, length us, event | category | flops | bytes accessed | tf_op | source)
XLA Modules:
  0.0 60.4 jit_solution(12790631843980858415)
XLA Ops:
  0.6 0.0 copy-start.3
  0.6 0.0 copy-start.4
  0.7 0.0 copy-start.1
  0.7 0.0 copy-start.2
  0.7 0.0 copy-start.5
  0.7 0.0 copy-start
  0.7 57.3 %step.1 = (f32[1,3072]{1,0:T(1,128)}, f32[1,3072]{1,0:T(1,128)}, f32[1,4096]{1,0:T(1,128)}, f32[1,128]{1,0:T(1,128)}, f32[1,1]{1,0:T(1,128)}) custom-call(f32[1,3072]{1,0:T(1,128)} %bitcast.19, f32[1,3072]{1,0:T(1,128)} %bitcast.23, f32[1,3072]{1,0:T(1,128)} %bitcast.34, s32[2,3072]{1,0:T(2,128)} %ends_all.1, f32[1,4096]{1,0:T(1,128)} %bitcast.30, ...), custom_call_target="tpu_custom_call" | custom-call | tf_op jit(solution)/shard_map/step/pallas_call | solution.py:483
  58.0 0.0 copy-done.3
  58.0 0.0 copy-done.4
  58.1 0.0 copy-done.1
  58.1 0.0 copy-done.2
  58.1 0.0 copy-done.5
  58.1 0.0 copy-done
  58.1 0.9 %while.15 = (f32[1,3072]{1,0:T(1,128)}, f32[1,3072]{1,0:T(1,128)}, f32[1,4096]{1,0:T(1,128)}, f32[1,128]{1,0:T(1,128)}, f32[1,1]{1,0:T(1,128)}, /*index=5*/f32[1...) while((f32[1,3072]{1,0:T(1,128)}, f32[1,3072]{1,0:T(1,128)}, ...), condition=%region_3.4_spmd, body=%region_0.3_spmd | while | flops 1490954 | bytes 30777616 | solution.py:518
  59.0 1.4 %hand_over.1 = (f32[1,3072]{1,0:T(1,128)}, f32[1,3072]{1,0:T(1,128)}, f32[1,4096]{1,0:T(1,128)}, f32[1,2]{1,0:T(1,128)}) custom-call(f32[1,3072]{1,0:T(1,128)} %get-tuple-element.92.step_primal, f32[1,3072]{1,0:T(1,128)} %get-tuple-element.93.step_slack, f32[1,4096]{1,0:T(1,128)} %get-tuple-element.94.step_dual, f32[1,128]{1,0:T(1,128)} %get-tuple-element.95.lengths), custom_call_target="tpu_custom_call" | custom-call | tf_op jit(solution)/shard_map/hand_over/pallas_call | solution.py:519
Async XLA Ops:
  0.6 57.4 %copy-start.3 = (f32[4096]{0:T(1024)S(1)}, f32[4096]{0:T(1024)}, u32[]{:S(2)}) copy-start(f32[4096]{0:T(1024)} %param.12) | copy-start | bytes 49156
  0.6 57.4 %copy-start.4 = (f32[4096]{0:T(1024)S(1)}, f32[4096]{0:T(1024)}, u32[]{:S(2)}) copy-start(f32[4096]{0:T(1024)} %param.13) | copy-start | bytes 49156
  0.7 57.4 %copy-start.1 = (f32[3072]{0:T(1024)S(1)}, f32[3072]{0:T(1024)}, u32[]{:S(2)}) copy-start(f32[3072]{0:T(1024)} %param.9) | copy-start | bytes 36868
  0.7 57.4 %copy-start.2 = (f32[3072]{0:T(1024)S(1)}, f32[3072]{0:T(1024)}, u32[]{:S(2)}) copy-start(f32[3072]{0:T(1024)} %param.10) | copy-start | bytes 36868
  0.7 57.4 %copy-start.5 = (f32[3072]{0:T(1024)S(1)}, f32[3072]{0:T(1024)}, u32[]{:S(2)}) copy-start(f32[3072]{0:T(1024)} %param.11) | copy-start | bytes 36868
  0.7 57.4 %copy-start = (s32[2,3072]{1,0:T(2,128)S(1)}, s32[2,3072]{1,0:T(2,128)}, u32[]{:S(2)}) copy-start(s32[2,3072]{1,0:T(2,128)} %ends_all.1) | copy-start | bytes 73732

commit v5 on v4

--- a/solution.py
+++ b/solution.py
@@ -16,7 +16,7 @@
 BS = 256
 PLANE = 32
 DEPTH = 8
-SLOTS = 32
+SLOTS = 20
 CHUNK = 512
 
 
@@ -35,12 +35,16 @@
     return high, middle, rest - middle
 
 
-def contract_lanes(a, b):
-    return lax.dot_general(a, b, (((1,), (1,)), ((), ())), preferred_element_type=f32)
+def multiply(a, b):
+    return jnp.dot(a, b, preferred_element_type=f32)
 
 
 def rows_of(shape):
     return lax.broadcasted_iota(jnp.int32, shape, 0)
+
+
+def lanes_of(shape):
+    return lax.broadcasted_iota(jnp.int32, shape, 1)
 
 
 def build_selector(selector, place):
@@ -49,14 +53,26 @@
         selector[:, at] = jnp.where(rows_of((BS, 256)) == place[:, at], 1.0, 0.0).astype(bf16)
 
 
-def to_buses(values, block, selector):
+def one_hot_rows(row, width):
+    diagonal = jnp.where(rows_of((128, 128)) == lanes_of((128, 128)), row, 0.0).astype(bf16)
+    value = multiply(diagonal, jnp.ones((128, width), bf16))
+    return jnp.where(value == lanes_of((128, width)).astype(f32), 1.0, 0.0).astype(bf16)
+
+
+def build_line_selector(selector, place):
+    for j in range(place.shape[1] // 128):
+        at = slice(128 * j, 128 * (j + 1))
+        selector[at, :] = one_hot_rows(place[:, at].astype(f32), BS)
+
+
+def to_buses(values, block, line_selector):
     total = None
     pieces = [piece for v in values for piece in split3(v)]
     for j in range(block.shape[1] // CHUNK):
         at = slice(CHUNK * j, CHUNK * (j + 1))
         here = rows_of((PLANE, CHUNK)) == block[:, at]
         left = jnp.concatenate([jnp.where(here, p[:, at], 0.0).astype(bf16) for p in pieces], axis=0)
-        part = contract_lanes(left, selector[:, at])
+        part = multiply(left, line_selector[at, :])
         total = part if total is None else total + part
     sums = [total[PLANE * k : PLANE * (k + 1)] for k in range(len(pieces))]
     return [sums[3 * q] + sums[3 * q + 1] + sums[3 * q + 2] for q in range(len(values))]
@@ -221,7 +237,7 @@
         code = jnp.where(rank < SLOTS, rank + shift, -1.0)
         slots = jnp.where(rows_of((128, 256)).astype(f32) == code, 1.0, 0.0).astype(bf16)
         left = jnp.concatenate([jnp.where(here, v[:, at], 0.0).astype(bf16) for v in values], axis=0)
-        piece = contract_lanes(left, slots)
+        piece = lax.dot_general(left, slots, (((1,), (1,)), ((), ())), preferred_element_type=f32)
         packed = piece if packed is None else packed + piece
     packed = [packed[PLANE * k : PLANE * (k + 1)] for k in range(len(values))]
     return packed, jnp.max(carry, axis=0, keepdims=True)
@@ -229,32 +245,30 @@
 
 def bucket_lines(msg_in):
     group = 128 // SLOTS
-
-    def candidates(g, at):
-        return sum(msg_in[group * g + k, :, at] for k in range(1, group)) + msg_in[group * g, :, at]
-
+    near = rows_of((BS, 128)).astype(f32)
+    sides = []
+    for first in range(0, PLANE, group):
+        rows = msg_in[first, :, 256:640]
+        for k in range(first + 1, min(first + group, PLANE)):
+            rows = rows + msg_in[k, :, 256:640]
+        p, q, d = rows[:, 0:128], rows[:, 128:256], rows[:, 256:384]
+        here = near == p
+        left = [jnp.where(here, piece, 0.0).astype(bf16) for piece in split3(d)]
+        sides.append((left, one_hot_rows(q, BS)))
     total = None
-    near = rows_of((BS, 128)).astype(f32)
-    for g in range(PLANE // group):
-        p, q, d = (candidates(g, slice(256 + 128 * k, 384 + 128 * k)) for k in range(3))
-        from_here, to_here = near == p, near == q
-        right_side = jnp.concatenate(
-            [jnp.where(to_here, 1.0, 0.0).astype(bf16), jnp.where(from_here, 1.0, 0.0).astype(bf16)], axis=1
-        )
-        for piece in split3(d):
-            left = jnp.concatenate(
-                [jnp.where(from_here, piece, 0.0).astype(bf16), jnp.where(to_here, piece, 0.0).astype(bf16)], axis=1
-            )
-            add = contract_lanes(left, right_side)
+    for g in range(0, len(sides), 2):
+        right = jnp.concatenate([side[1] for side in sides[g : g + 2]], axis=0)
+        for k in range(3):
+            add = multiply(jnp.concatenate([side[0][k] for side in sides[g : g + 2]], axis=1), right)
             total = add if total is None else total + add
-    return total
+    return total + total.T
 
 
 def step_kernel(
     total_lines, given,
     primal_all, slacks_all, cost_all, ends_all, bus_dual_all, demand_all, normal,
     step_primal, step_slack, step_dual, lengths, fullest,
-    primal, slacks, cost, ends, bus_dual, demand, selector, partner, msg, msg_in, diff0, diff0_in, part0, part0_in, block_in, work, dual_res,
+    primal, slacks, cost, ends, bus_dual, demand, selector, line_selector, partner, msg, msg_in, diff0, diff0_in, part0, part0_in, block_in, work, dual_res, split,
     solved, solved_in, diff, diff_in, part, part_in, solved2, solved2_in, diff2, diff2_in, final, final_in, last, last_in,
     in_sem, fixed_sem, pair_sem, msg_sem, diff0_sem, part0_sem,
     solved_sem, diff_sem, part_sem, solved2_sem, diff2_sem, last_sem, final_sem,
@@ -286,7 +300,7 @@
     lane1 = lax.broadcasted_iota(jnp.int32, (1, 128), 1)
     copies[0].wait()
     start, end, place, block = endpoint_rows(ends, z)
-    build_selector(selector, place)
+    build_line_selector(line_selector, place)
     copies[1].wait()
     copies[2].wait()
     x, s = primal[...], slacks[...]
@@ -298,7 +312,7 @@
     packed, most = buckets(
         owner, [place[:, :half].astype(f32), place[:, half:].astype(f32), *split3(scaling)], shift
     )
-    (ends_sum,) = to_buses([jnp.concatenate([scaling, scaling], axis=1)], block, selector)
+    (ends_sum,) = to_buses([jnp.concatenate([scaling, scaling], axis=1)], block, line_selector)
     whole = jnp.concatenate(
         [ends_sum, packed[0], packed[1], packed[2] + packed[3] + packed[4], jnp.broadcast_to(gap, (PLANE, 128))],
         axis=1,
@@ -315,6 +329,7 @@
     pair.start()
     send_plane(lambda b: msg.at[b], msg.at[at_home], source, msg_in, msg_sem, li, z, c)
 
+    build_selector(selector, place)
     pair.wait()
     mine_dual = jnp.concatenate([bus_dual[:, BS * k : BS * (k + 1)] for k in range(16)], axis=0)
     other_dual = jnp.concatenate([partner[:, BS * k : BS * (k + 1)] for k in range(16)], axis=0)
@@ -325,6 +340,9 @@
     diff0[:, half:] = jnp.broadcast_to(most, (1, 128))
     send_depth(diff0, diff0_in, diff0_sem, li, z, c)
 
+    (sums,) = to_buses([jnp.concatenate([inverse, -inverse], axis=1)], block, line_selector)
+    for b in range(PLANE):
+        part0[b, :, 256:512] = sums[b : b + 1]
     wait_bytes(msg_in, msg_sem.at[1])
     sums = sum_slots(msg_in, slice(0, 256))
     gap0 = sum_slots(msg_in, slice(640, 768))[:, 0:1]
@@ -345,12 +363,10 @@
         for k in range(1, DEPTH):
             most = jnp.maximum(most, diff0_in[k, :, half:])
         flow = scaling * residual
-        sums = to_buses(
-            [jnp.concatenate([flow, -flow], axis=1), jnp.concatenate([inverse, -inverse], axis=1)], block, selector
-        )
-        whole = jnp.concatenate([*sums, jnp.broadcast_to(most, (PLANE, 128))], axis=1)
+        (sums,) = to_buses([jnp.concatenate([flow, -flow], axis=1)], block, line_selector)
         for b in range(PLANE):
-            part0[b] = whole[b : b + 1]
+            part0[b, :, 0:256] = sums[b : b + 1]
+            part0[b, :, 512:640] = most
         send_plane(lambda b: part0.at[b], part0.at[at_home], source, part0_in, part0_sem, li, z, c)
 
     invert(work, first_right_side)
@@ -364,6 +380,8 @@
 
     solved[...] = solve(right)
     send_plane(lambda b: solved, solved, at_home, solved_in, solved_sem, li, z, c)
+    for k, piece in enumerate(split3(work[...])):
+        split[k] = piece.astype(bf16)
     wait_bytes(solved_in, solved_sem.at[1])
     table = jnp.concatenate([solved_in[b] for b in range(PLANE)], axis=0)
     diff[...] = to_lines(table, block, selector)
@@ -373,7 +391,7 @@
     affine_primal = -x - scaling * affine_slack
     cross = affine_primal * affine_slack
     extra = cross / s
-    (sums,) = to_buses([jnp.concatenate([extra, -extra], axis=1)], block, selector)
+    (sums,) = to_buses([jnp.concatenate([extra, -extra], axis=1)], block, line_selector)
     scalars = [
         longest_step(x, affine_primal),
         longest_step(s, affine_slack),
@@ -399,7 +417,13 @@
     gap_affine = gap0 + take_p * tail[:, 2:3] + take_d * tail[:, 3:4] + take_p * take_d * tail[:, 4:5]
     ratio = gap_affine / gap0
     aim = ratio * ratio * ratio * (gap0 / total_lines)
-    solved2[...] = solve(right - aim * third + added[:, :256])
+    right = right - aim * third + added[:, :256]
+    high, middle, low = split3(jnp.broadcast_to(right, (8, BS)))
+    three = jnp.concatenate([high, middle, low], axis=0).astype(bf16)
+    by_high, by_middle, by_low = multiply(three, split[0]), multiply(three[0:16], split[1]), multiply(three[0:8], split[2])
+    solved2[...] = (
+        by_high[0:1] + (by_high[8:9] + by_middle[0:1]) + (by_high[16:17] + by_middle[8:9] + by_low[0:1])
+    )
     send_plane(lambda b: solved2, solved2, at_home, solved2_in, solved2_sem, li, z, c)
     wait_bytes(solved2_in, solved2_sem.at[1])
     table = jnp.concatenate([solved2_in[b] for b in range(PLANE)], axis=0)
@@ -487,12 +511,12 @@
         out_specs=tuple(vmem(5)),
         scratch_shapes=[pltpu.VMEM((1, half), f32)] * 3
         + [pltpu.VMEM((2, half), jnp.int32), pltpu.VMEM((1, buses_here), f32), pltpu.VMEM((1, BS), f32)]
-        + [pltpu.VMEM((BS, lines_here), bf16), pltpu.VMEM((1, buses_here), f32)]
+        + [pltpu.VMEM((BS, lines_here), bf16), pltpu.VMEM((lines_here, BS), bf16), pltpu.VMEM((1, buses_here), f32)]
         + buckets_of(768)
         + exchange(DEPTH, half + 128)
         + buckets_of(640)
         + [pltpu.VMEM((BS, BS), f32)] * 2
-        + [pltpu.VMEM((1, half), f32)]
+        + [pltpu.VMEM((1, half), f32), pltpu.VMEM((3, BS, BS), bf16)]
         + exchange(PLANE, BS)
         + exchange(DEPTH, half)
         + buckets_of(384)

time: 60.6 us -> 58.4 us (0.964)
  Pallas kernels: 58.7 us -> 56.8 us
    pallas_call x1, Pallas kernels: 57.3 us -> 55.4 us  [whole_step(): pl.pallas_call(functools.partial(step_kernel, total_lines, given), out_sh...]
where the time goes in v5:
time: 58.4 us; the launch traced here: 58.2 us
  Pallas kernels  56.8 us (97%)
  between operations  0.74 us (1%)
  loops' own time  0.69 us (1%)
    pallas_call x1, Pallas kernels, whole_step(): pl.pallas_call(functools.partial(step_kernel, total_lines, given), out_sh...  55.4 us
    pallas_call x1, Pallas kernels, per_device(): pl.pallas_call(hand_over, out_shape=tuple((struct(*a.shape) for a in step...  1.37 us

profile of v5, /device:TPU:1, one launch (start us, length us, event | category | flops | bytes accessed | tf_op | source)
XLA Modules:
  0.0 58.2 jit_solution(5565305565389731885)
XLA Ops:
  0.6 0.0 copy-start.3
  0.6 0.0 copy-start.4
  0.7 0.0 copy-start.1
  0.7 0.0 copy-start.2
  0.7 0.0 copy-start.5
  0.7 0.0 copy-start
  0.7 55.4 %step.1 = (f32[1,3072]{1,0:T(1,128)}, f32[1,3072]{1,0:T(1,128)}, f32[1,4096]{1,0:T(1,128)}, f32[1,128]{1,0:T(1,128)}, f32[1,1]{1,0:T(1,128)}) custom-call(f32[1,3072]{1,0:T(1,128)} %bitcast.19, f32[1,3072]{1,0:T(1,128)} %bitcast.23, f32[1,3072]{1,0:T(1,128)} %bitcast.34, s32[2,3072]{1,0:T(2,128)} %ends_all.1, f32[1,4096]{1,0:T(1,128)} %bitcast.30, ...), custom_call_target="tpu_custom_call" | custom-call | tf_op jit(solution)/shard_map/step/pallas_call | solution.py:507
  56.1 0.0 copy-done.3
  56.1 0.0 copy-done.4
  56.1 0.0 copy-done.1
  56.1 0.0 copy-done.2
  56.1 0.0 copy-done.5
  56.1 0.0 copy-done
  56.2 0.7 %while.15 = (f32[1,3072]{1,0:T(1,128)}, f32[1,3072]{1,0:T(1,128)}, f32[1,4096]{1,0:T(1,128)}, f32[1,128]{1,0:T(1,128)}, f32[1,1]{1,0:T(1,128)}, /*index=5*/f32[1...) while((f32[1,3072]{1,0:T(1,128)}, f32[1,3072]{1,0:T(1,128)}, ...), condition=%region_3.4_spmd, body=%region_0.3_spmd | while | flops 1490954 | bytes 30777616 | solution.py:542
  56.9 1.4 %hand_over.1 = (f32[1,3072]{1,0:T(1,128)}, f32[1,3072]{1,0:T(1,128)}, f32[1,4096]{1,0:T(1,128)}, f32[1,2]{1,0:T(1,128)}) custom-call(f32[1,3072]{1,0:T(1,128)} %get-tuple-element.92.step_primal, f32[1,3072]{1,0:T(1,128)} %get-tuple-element.93.step_slack, f32[1,4096]{1,0:T(1,128)} %get-tuple-element.94.step_dual, f32[1,128]{1,0:T(1,128)} %get-tuple-element.95.lengths), custom_call_target="tpu_custom_call" | custom-call | tf_op jit(solution)/shard_map/hand_over/pallas_call | solution.py:543
Async XLA Ops:
  0.6 55.5 %copy-start.3 = (f32[4096]{0:T(1024)S(1)}, f32[4096]{0:T(1024)}, u32[]{:S(2)}) copy-start(f32[4096]{0:T(1024)} %param.12) | copy-start | bytes 49156
  0.6 55.5 %copy-start.4 = (f32[4096]{0:T(1024)S(1)}, f32[4096]{0:T(1024)}, u32[]{:S(2)}) copy-start(f32[4096]{0:T(1024)} %param.13) | copy-start | bytes 49156
  0.7 55.5 %copy-start.1 = (f32[3072]{0:T(1024)S(1)}, f32[3072]{0:T(1024)}, u32[]{:S(2)}) copy-start(f32[3072]{0:T(1024)} %param.9) | copy-start | bytes 36868
  0.7 55.5 %copy-start.2 = (f32[3072]{0:T(1024)S(1)}, f32[3072]{0:T(1024)}, u32[]{:S(2)}) copy-start(f32[3072]{0:T(1024)} %param.10) | copy-start | bytes 36868
  0.7 55.5 %copy-start.5 = (f32[3072]{0:T(1024)S(1)}, f32[3072]{0:T(1024)}, u32[]{:S(2)}) copy-start(f32[3072]{0:T(1024)} %param.11) | copy-start | bytes 36868
  0.7 55.5 %copy-start = (s32[2,3072]{1,0:T(2,128)S(1)}, s32[2,3072]{1,0:T(2,128)}, u32[]{:S(2)}) copy-start(s32[2,3072]{1,0:T(2,128)} %ends_all.1) | copy-start | bytes 73732

commit v6 on v5

--- a/solution.py
+++ b/solution.py
@@ -16,6 +16,7 @@
 BS = 256
 PLANE = 32
 DEPTH = 8
+LANE_STEP = 42
 SLOTS = 20
 CHUNK = 512
 
@@ -244,16 +245,27 @@
 
 
 def bucket_lines(msg_in):
-    group = 128 // SLOTS
     near = rows_of((BS, 128)).astype(f32)
+    rows = [msg_in[k, :, 256:384] + msg_in[k + 1, :, 256:384] for k in range(0, PLANE, 2)]
+    here = jnp.concatenate(rows, axis=0)
+    up, up2 = pltpu.roll(here, LANE_STEP, 1), pltpu.roll(here, 2 * LANE_STEP, 1)
+    down, down2 = pltpu.roll(here, 128 - LANE_STEP, 1), pltpu.roll(here, 128 - 2 * LANE_STEP, 1)
+    lane = lanes_of((1, 128))
+
+    def joined(parts, first):
+        row = jnp.zeros((1, 128), f32)
+        for k in (2, 1, 0):
+            if first + k < len(rows):
+                row = jnp.where(lane < LANE_STEP * (k + 1), parts[k][first + k : first + k + 1], row)
+            else:
+                row = jnp.where(lane < LANE_STEP * (k + 1), 0.0, row)
+        return row
+
     sides = []
-    for first in range(0, PLANE, group):
-        rows = msg_in[first, :, 256:640]
-        for k in range(first + 1, min(first + group, PLANE)):
-            rows = rows + msg_in[k, :, 256:640]
-        p, q, d = rows[:, 0:128], rows[:, 128:256], rows[:, 256:384]
-        here = near == p
-        left = [jnp.where(here, piece, 0.0).astype(bf16) for piece in split3(d)]
+    for first in range(0, len(rows), 3):
+        p, q, d = joined((here, up, up2), first), joined((down, here, up), first), joined((down2, down, here), first)
+        mark = near == p
+        left = [jnp.where(mark, piece, 0.0).astype(bf16) for piece in split3(d)]
         sides.append((left, one_hot_rows(q, BS)))
     total = None
     for g in range(0, len(sides), 2):
@@ -271,10 +283,9 @@
     primal, slacks, cost, ends, bus_dual, demand, selector, line_selector, partner, msg, msg_in, diff0, diff0_in, part0, part0_in, block_in, work, dual_res, split,
     solved, solved_in, diff, diff_in, part, part_in, solved2, solved2_in, diff2, diff2_in, final, final_in, last, last_in,
     in_sem, fixed_sem, pair_sem, msg_sem, diff0_sem, part0_sem,
-    solved_sem, diff_sem, part_sem, solved2_sem, diff2_sem, last_sem, final_sem,
+    solved_sem, diff_sem, part_sem, solved2_sem, diff2_sem, last_sem, final_sem, out_sem,
 ):
     li, z, c = position()
-    greet(li, z, c)
     half = primal.shape[1]
     mine = pl.ds(pl.multiple_of(c * half, half), half)
     own_buses = pl.ds(pl.multiple_of(li * BS, BS), BS)
@@ -295,6 +306,7 @@
         copy.start()
     own = pltpu.make_async_copy(normal if given else normal.at[li], block_in, fixed_sem)
     own.start()
+    greet(li, z, c)
     at_home = c * 16 + li
     source = 2 * li + c
     lane1 = lax.broadcasted_iota(jnp.int32, (1, 128), 1)
@@ -308,15 +320,15 @@
     inverse = 1.0 / s
     gap = jnp.sum(x * s, axis=1, keepdims=True)
     owner = jnp.where((start >> 8) == (end >> 8), block[:, :half], -1)
-    shift = (SLOTS * lax.rem(source, 128 // SLOTS)).astype(f32)
+    shift = (SLOTS * lax.rem(source, 2)).astype(f32)
     packed, most = buckets(
         owner, [place[:, :half].astype(f32), place[:, half:].astype(f32), *split3(scaling)], shift
     )
     (ends_sum,) = to_buses([jnp.concatenate([scaling, scaling], axis=1)], block, line_selector)
-    whole = jnp.concatenate(
-        [ends_sum, packed[0], packed[1], packed[2] + packed[3] + packed[4], jnp.broadcast_to(gap, (PLANE, 128))],
-        axis=1,
-    )
+    row = packed[0] + pltpu.roll(packed[1], LANE_STEP, 1)
+    row = row + pltpu.roll(packed[2] + packed[3] + packed[4], 2 * LANE_STEP, 1)
+    row = jnp.where(lane1 == 127, gap, row)
+    whole = jnp.concatenate([ends_sum, row], axis=1)
     for b in range(PLANE):
         msg[b] = whole[b : b + 1]
     for copy in copies[3:]:
@@ -345,7 +357,7 @@
         part0[b, :, 256:512] = sums[b : b + 1]
     wait_bytes(msg_in, msg_sem.at[1])
     sums = sum_slots(msg_in, slice(0, 256))
-    gap0 = sum_slots(msg_in, slice(640, 768))[:, 0:1]
+    gap0 = sum_slots(msg_in, slice(256, 384))[:, 127:128]
     own.wait()
     if given:
         work[...] = block_in[...]
@@ -430,33 +442,35 @@
     diff2[...] = to_lines(table, block, selector)
     send_depth(diff2, diff2_in, diff2_sem, li, z, c)
     for b in range(16):
-        step_dual[:, BS * b : BS * (b + 1)] = solved2_in[16 * c + b]
+        pltpu.make_async_copy(solved2_in.at[16 * c + b], step_dual.at[:, pl.ds(BS * b, BS)], out_sem.at[2]).start()
     wait_bytes(diff2_in, diff2_sem.at[1])
     slack = dual_res[...] - sum_slots(diff2_in, slice(0, half))
     primal_step = (aim - x * s - cross) / s - scaling * slack
     last[...] = jnp.where(lane1 == 0, longest_step(x, primal_step), longest_step(s, slack))
-    final[0:1] = primal_step
-    final[1:2] = slack
+    final[0] = primal_step
+    final[1] = slack
     send_plane(lambda b: last, last, source, last_in, last_sem, li, z, c)
     pair2 = pltpu.make_async_remote_copy(
         final, final_in, final_sem.at[0], final_sem.at[1], device_id=(li, 2 * z + 1 - c), device_id_type=MESH
     )
     pair2.start()
-    step_primal[:, mine] = primal_step
-    step_slack[:, mine] = slack
+    for k, out in enumerate((step_primal, step_slack)):
+        pltpu.make_async_copy(final.at[k], out.at[:, mine], out_sem.at[k]).start()
     most = part0_in[0, :, 512:]
     for k in range(1, PLANE):
         most = jnp.maximum(most, part0_in[k, :, 512:])
     fullest[...] = most[:, 0:1]
     pair2.wait()
     other = pl.ds(pl.multiple_of((1 - c) * half, half), half)
-    step_primal[:, other] = final_in[0:1]
-    step_slack[:, other] = final_in[1:2]
+    for k, out in enumerate((step_primal, step_slack)):
+        pltpu.make_async_copy(final_in.at[k], out.at[:, other], out_sem.at[k]).start()
     for recv, sems in (
         (msg_in, msg_sem), (diff0_in, diff0_sem), (part0_in, part0_sem), (solved_in, solved_sem), (diff_in, diff_sem),
         (part_in, part_sem), (solved2_in, solved2_sem), (diff2_in, diff2_sem), (last_in, last_sem),
     ):
         wait_bytes(recv.at[pl.ds(0, recv.shape[0] - 1)], sems.at[0])
+    for k, out in enumerate((step_primal, step_slack, step_dual)):
+        wait_bytes(out, out_sem.at[k])
     wait_bytes(last_in, last_sem.at[1])
     least = last_in[0]
     for k in range(1, PLANE):
@@ -508,11 +522,11 @@
         functools.partial(step_kernel, total_lines, given),
         out_shape=(struct(1, lines_here), struct(1, lines_here), struct(1, buses_here), struct(1, 128), struct(1, 1)),
         in_specs=[pl.BlockSpec(memory_space=pl.ANY)] * 7,
-        out_specs=tuple(vmem(5)),
+        out_specs=(pl.BlockSpec(memory_space=pl.ANY),) * 3 + tuple(vmem(2)),
         scratch_shapes=[pltpu.VMEM((1, half), f32)] * 3
         + [pltpu.VMEM((2, half), jnp.int32), pltpu.VMEM((1, buses_here), f32), pltpu.VMEM((1, BS), f32)]
         + [pltpu.VMEM((BS, lines_here), bf16), pltpu.VMEM((lines_here, BS), bf16), pltpu.VMEM((1, buses_here), f32)]
-        + buckets_of(768)
+        + buckets_of(384)
         + exchange(DEPTH, half + 128)
         + buckets_of(640)
         + [pltpu.VMEM((BS, BS), f32)] * 2
@@ -522,10 +536,11 @@
         + buckets_of(384)
         + exchange(PLANE, BS)
         + exchange(DEPTH, half)
-        + [pltpu.VMEM((2, half), f32)] * 2
+        + [pltpu.VMEM((2, 1, half), f32)] * 2
         + exchange(PLANE, 128)
         + [dma((6,)), dma]
-        + [dma((2,))] * 11,
+        + [dma((2,))] * 11
+        + [dma((3,))],
         compiler_params=pltpu.CompilerParams(collective_id=int(given), has_side_effects=True),
         name="step_given" if given else "step",
     )(*args, normal)

time: 58.4 us -> 58.6 us (level)
  no operation moved by 1% of the time
where the time goes in v6:
time: 58.6 us; the launch traced here: 58.5 us
  Pallas kernels  57 us (97%)
  between operations  0.74 us (1%)
  loops' own time  0.69 us (1%)
    pallas_call x1, Pallas kernels, whole_step(): pl.pallas_call(functools.partial(step_kernel, total_lines, given), out_sh...  55.6 us
    pallas_call x1, Pallas kernels, per_device(): pl.pallas_call(hand_over, out_shape=tuple((struct(*a.shape) for a in step...  1.37 us

profile of v6, /device:TPU:1, one launch (start us, length us, event | category | flops | bytes accessed | tf_op | source)
XLA Modules:
  0.0 58.5 jit_solution(4782102788374975971)
XLA Ops:
  0.6 0.0 copy-start.3
  0.6 0.0 copy-start.4
  0.7 0.0 copy-start.1
  0.7 0.0 copy-start.2
  0.7 0.0 copy-start.5
  0.7 0.0 copy-start
  0.7 55.6 %step.1 = (f32[1,3072]{1,0:T(1,128)}, f32[1,3072]{1,0:T(1,128)}, f32[1,4096]{1,0:T(1,128)}, f32[1,128]{1,0:T(1,128)}, f32[1,1]{1,0:T(1,128)}) custom-call(f32[1,3072]{1,0:T(1,128)} %bitcast.19, f32[1,3072]{1,0:T(1,128)} %bitcast.23, f32[1,3072]{1,0:T(1,128)} %bitcast.34, s32[2,3072]{1,0:T(2,128)} %ends_all.1, f32[1,4096]{1,0:T(1,128)} %bitcast.30, ...), custom_call_target="tpu_custom_call" | custom-call | tf_op jit(solution)/shard_map/step/pallas_call | solution.py:521
  56.3 0.0 copy-done.3
  56.3 0.0 copy-done.4
  56.4 0.0 copy-done.1
  56.4 0.0 copy-done.2
  56.4 0.0 copy-done.5
  56.4 0.0 copy-done
  56.4 0.7 %while.15 = (f32[1,3072]{1,0:T(1,128)}, f32[1,3072]{1,0:T(1,128)}, f32[1,4096]{1,0:T(1,128)}, f32[1,128]{1,0:T(1,128)}, f32[1,1]{1,0:T(1,128)}, /*index=5*/f32[1...) while((f32[1,3072]{1,0:T(1,128)}, f32[1,3072]{1,0:T(1,128)}, ...), condition=%region_3.4_spmd, body=%region_0.3_spmd | while | flops 1490954 | bytes 30777616 | solution.py:557
  57.1 1.4 %hand_over.1 = (f32[1,3072]{1,0:T(1,128)}, f32[1,3072]{1,0:T(1,128)}, f32[1,4096]{1,0:T(1,128)}, f32[1,2]{1,0:T(1,128)}) custom-call(f32[1,3072]{1,0:T(1,128)} %get-tuple-element.92.step_primal, f32[1,3072]{1,0:T(1,128)} %get-tuple-element.93.step_slack, f32[1,4096]{1,0:T(1,128)} %get-tuple-element.94.step_dual, f32[1,128]{1,0:T(1,128)} %get-tuple-element.95.lengths), custom_call_target="tpu_custom_call" | custom-call | tf_op jit(solution)/shard_map/hand_over/pallas_call | solution.py:558
Async XLA Ops:
  0.6 55.7 %copy-start.3 = (f32[4096]{0:T(1024)S(1)}, f32[4096]{0:T(1024)}, u32[]{:S(2)}) copy-start(f32[4096]{0:T(1024)} %param.12) | copy-start | bytes 49156
  0.6 55.7 %copy-start.4 = (f32[4096]{0:T(1024)S(1)}, f32[4096]{0:T(1024)}, u32[]{:S(2)}) copy-start(f32[4096]{0:T(1024)} %param.13) | copy-start | bytes 49156
  0.7 55.7 %copy-start.1 = (f32[3072]{0:T(1024)S(1)}, f32[3072]{0:T(1024)}, u32[]{:S(2)}) copy-start(f32[3072]{0:T(1024)} %param.9) | copy-start | bytes 36868
  0.7 55.7 %copy-start.2 = (f32[3072]{0:T(1024)S(1)}, f32[3072]{0:T(1024)}, u32[]{:S(2)}) copy-start(f32[3072]{0:T(1024)} %param.10) | copy-start | bytes 36868
  0.7 55.7 %copy-start.5 = (f32[3072]{0:T(1024)S(1)}, f32[3072]{0:T(1024)}, u32[]{:S(2)}) copy-start(f32[3072]{0:T(1024)} %param.11) | copy-start | bytes 36868
  0.7 55.7 %copy-start = (s32[2,3072]{1,0:T(2,128)S(1)}, s32[2,3072]{1,0:T(2,128)}, u32[]{:S(2)}) copy-start(s32[2,3072]{1,0:T(2,128)} %ends_all.1) | copy-start | bytes 73732

commit v7 on v6

--- a/solution.py
+++ b/solution.py
@@ -366,9 +366,12 @@
         work[...] = block_in[...] + jnp.where(diagonal, sums, 0.0) - bucket_lines(msg_in)
 
     def first_right_side(panel):
-        if panel != 1:
+        if panel == 1:
+            send_plane(
+                lambda b: part0.at[b], part0.at[at_home], source, part0_in, part0_sem, li, z, c
+            )
+        if panel != 0:
             return
-        wait_bytes(diff0_in, diff0_sem.at[1])
         residual = cost[...] - sum_slots(diff0_in, slice(0, half)) - s
         dual_res[...] = residual
         most = diff0_in[0, :, half:]
@@ -379,12 +382,11 @@
         for b in range(PLANE):
             part0[b, :, 0:256] = sums[b : b + 1]
             part0[b, :, 512:640] = most
-        send_plane(lambda b: part0.at[b], part0.at[at_home], source, part0_in, part0_sem, li, z, c)
-
+
+    wait_bytes(diff0_in, diff0_sem.at[1])
     invert(work, first_right_side)
     wait_bytes(part0_in, part0_sem.at[1])
-    sums = sum_slots(part0_in, slice(0, 512))
-    right, third = demand[...] + sums[:, :256], sums[:, 256:]
+    right = demand[...] + sum_slots(part0_in, slice(0, 256))
 
     def solve(vector):
         wide = jnp.broadcast_to(vector, (8, BS))
@@ -394,6 +396,7 @@
     send_plane(lambda b: solved, solved, at_home, solved_in, solved_sem, li, z, c)
     for k, piece in enumerate(split3(work[...])):
         split[k] = piece.astype(bf16)
+    third = sum_slots(part0_in, slice(256, 512))
     wait_bytes(solved_in, solved_sem.at[1])
     table = jnp.concatenate([solved_in[b] for b in range(PLANE)], axis=0)
     diff[...] = to_lines(table, block, selector)
@@ -520,9 +523,9 @@
     buckets_of = lambda width: [pltpu.VMEM((PLANE, 1, width), f32)] * 2
     return pl.pallas_call(
         functools.partial(step_kernel, total_lines, given),
-        out_shape=(struct(1, lines_here), struct(1, lines_here), struct(1, buses_here), struct(1, 128), struct(1, 1)),
+        out_shape=tuple(pltpu.VMEM((1, n), f32) for n in (lines_here, lines_here, buses_here, 128, 1)),
         in_specs=[pl.BlockSpec(memory_space=pl.ANY)] * 7,
-        out_specs=(pl.BlockSpec(memory_space=pl.ANY),) * 3 + tuple(vmem(2)),
+        out_specs=tuple(vmem(5)),
         scratch_shapes=[pltpu.VMEM((1, half), f32)] * 3
         + [pltpu.VMEM((2, half), jnp.int32), pltpu.VMEM((1, buses_here), f32), pltpu.VMEM((1, BS), f32)]
         + [pltpu.VMEM((BS, lines_here), bf16), pltpu.VMEM((lines_here, BS), bf16), pltpu.VMEM((1, buses_here), f32)]

time: 58.6 us -> 57.2 us (0.976)
  Pallas kernels: 57 us -> 55.6 us
    pallas_call x1, Pallas kernels: 1.37 us -> 0.62 us  [per_device(): pl.pallas_call(hand_over, out_shape=tuple((struct(*a.shape) for a in step...]
    pallas_call x1, Pallas kernels: 55.6 us -> 55 us  [whole_step(): pl.pallas_call(functools.partial(step_kernel, total_lines, given), out_sh...]
where the time goes in v7:
time: 57.2 us; the launch traced here: 57.1 us
  Pallas kernels  55.6 us (97%)
  between operations  0.74 us (1%)
  loops' own time  0.69 us (1%)
    pallas_call x1, Pallas kernels, whole_step(): pl.pallas_call(functools.partial(step_kernel, total_lines, given), out_sh...  55 us

profile of v7, /device:TPU:1, one launch (start us, length us, event | category | flops | bytes accessed | tf_op | source)
XLA Modules:
  0.0 57.1 jit_solution(3226060118560997081)
XLA Ops:
  0.6 0.0 copy-start.3
  0.6 0.0 copy-start.4
  0.7 0.0 copy-start.1
  0.7 0.0 copy-start.2
  0.7 0.0 copy-start.5
  0.7 0.0 copy-start
  0.7 55.0 %step.1 = (f32[1,3072]{1,0:T(1,128)S(1)}, f32[1,3072]{1,0:T(1,128)S(1)}, f32[1,4096]{1,0:T(1,128)S(1)}, f32[1,128]{1,0:T(1,128)S(1)}, f32[1,1]{1,0:T(1,128)}) custom-call(f32[1,3072]{1,0:T(1,128)} %bitcast.19, f32[1,3072]{1,0:T(1,128)} %bitcast.23, f32[1,3072]{1,0:T(1,128)} %bitcast.34, s32[2,3072]{1,0:T(2,128)} %ends_all.1, f32[1,4096]{1,0:T(1,128)} %bitcast.30, ...), custom_call_target="tpu_custom_call" | custom-call | tf_op jit(solution)/shard_map/step/pallas_call | solution.py:524
  55.7 0.0 copy-done.3
  55.7 0.0 copy-done.4
  55.7 0.0 copy-done.1
  55.7 0.0 copy-done.2
  55.7 0.0 copy-done.5
  55.7 0.0 copy-done
  55.7 0.7 %while.15 = (f32[1,3072]{1,0:T(1,128)S(1)}, f32[1,3072]{1,0:T(1,128)S(1)}, f32[1,4096]{1,0:T(1,128)S(1)}, f32[1,128]{1,0:T(1,128)S(1)}, f32[1,1]{1,0:T(1,128)}, ...) while((f32[1,3072]{1,0:T(1,128)S(1)}, ...), condition=%region_3.4_spmd, body=%region_0.3_spmd | while | flops 1490954 | bytes 30777616 | solution.py:560
  56.4 0.6 %hand_over.1 = (f32[1,3072]{1,0:T(1,128)}, f32[1,3072]{1,0:T(1,128)}, f32[1,4096]{1,0:T(1,128)}, f32[1,2]{1,0:T(1,128)}) custom-call(f32[1,3072]{1,0:T(1,128)S(1)} %get-tuple-element.92.step_primal, f32[1,3072]{1,0:T(1,128)S(1)} %get-tuple-element.93.step_slack, f32[1,4096]{1,0:T(1,128)S(1)} %get-tuple-element.94.step_dual, ...), custom_call_target="tpu_custom_call" | custom-call | tf_op jit(solution)/shard_map/hand_over/pallas_call | solution.py:561
Async XLA Ops:
  0.6 55.0 %copy-start.3 = (f32[4096]{0:T(1024)S(1)}, f32[4096]{0:T(1024)}, u32[]{:S(2)}) copy-start(f32[4096]{0:T(1024)} %param.12) | copy-start | bytes 49156
  0.6 55.0 %copy-start.4 = (f32[4096]{0:T(1024)S(1)}, f32[4096]{0:T(1024)}, u32[]{:S(2)}) copy-start(f32[4096]{0:T(1024)} %param.13) | copy-start | bytes 49156
  0.7 55.0 %copy-start.1 = (f32[3072]{0:T(1024)S(1)}, f32[3072]{0:T(1024)}, u32[]{:S(2)}) copy-start(f32[3072]{0:T(1024)} %param.9) | copy-start | bytes 36868
  0.7 55.0 %copy-start.2 = (f32[3072]{0:T(1024)S(1)}, f32[3072]{0:T(1024)}, u32[]{:S(2)}) copy-start(f32[3072]{0:T(1024)} %param.10) | copy-start | bytes 36868
  0.7 55.0 %copy-start.5 = (f32[3072]{0:T(1024)S(1)}, f32[3072]{0:T(1024)}, u32[]{:S(2)}) copy-start(f32[3072]{0:T(1024)} %param.11) | copy-start | bytes 36868
  0.7 55.0 %copy-start = (s32[2,3072]{1,0:T(2,128)S(1)}, s32[2,3072]{1,0:T(2,128)}, u32[]{:S(2)}) copy-start(s32[2,3072]{1,0:T(2,128)} %ends_all.1) | copy-start | bytes 73732

commit v8 on v7

--- a/solution.py
+++ b/solution.py
@@ -147,11 +147,15 @@
     pltpu.make_async_copy(ref, ref, sem).wait()
 
 
+def over_slots(combine, recv, at):
+    rows = [recv[k, :, at] for k in range(recv.shape[0])]
+    while len(rows) > 1:
+        rows = [combine(rows[k], rows[k + 1]) for k in range(0, len(rows), 2)]
+    return rows[0]
+
+
 def sum_slots(recv, at):
-    total = recv[0, :, at]
-    for s in range(1, recv.shape[0]):
-        total = total + recv[s, :, at]
-    return total
+    return over_slots(jnp.add, recv, at)
 
 
 def eliminate(pa, pb, off):
@@ -424,9 +428,7 @@
     wait_bytes(part_in, part_sem.at[1])
 
     added = sum_slots(part_in, slice(0, 384))
-    least = part_in[0, :, 256:384]
-    for k in range(1, PLANE):
-        least = jnp.minimum(least, part_in[k, :, 256:384])
+    least = over_slots(jnp.minimum, part_in, slice(256, 384))
     take_p, take_d = least[:, 0:1], least[:, 1:2]
     tail = added[:, 256:384]
     gap_affine = gap0 + take_p * tail[:, 2:3] + take_d * tail[:, 3:4] + take_p * take_d * tail[:, 4:5]
@@ -475,9 +477,7 @@
     for k, out in enumerate((step_primal, step_slack, step_dual)):
         wait_bytes(out, out_sem.at[k])
     wait_bytes(last_in, last_sem.at[1])
-    least = last_in[0]
-    for k in range(1, PLANE):
-        least = jnp.minimum(least, last_in[k])
+    least = over_slots(jnp.minimum, last_in, slice(0, 128))
     lengths[...] = damping * least
 
 

time: 57.2 us -> 57.1 us (level)
  no operation moved by 1% of the time
where the time goes in v8:
time: 57.1 us; the launch traced here: 57 us
  Pallas kernels  55.6 us (97%)
  between operations  0.74 us (1%)
  loops' own time  0.69 us (1%)
    pallas_call x1, Pallas kernels, whole_step(): pl.pallas_call(functools.partial(step_kernel, total_lines, given), out_sh...  54.9 us

profile of v8, /device:TPU:1, one launch (start us, length us, event | category | flops | bytes accessed | tf_op | source)
XLA Modules:
  0.0 57.0 jit_solution(2548951453039083336)
XLA Ops:
  0.6 0.0 copy-start.3
  0.6 0.0 copy-start.4
  0.7 0.0 copy-start.1
  0.7 0.0 copy-start.2
  0.7 0.0 copy-start.5
  0.7 0.0 copy-start
  0.7 54.9 %step.1 = (f32[1,3072]{1,0:T(1,128)S(1)}, f32[1,3072]{1,0:T(1,128)S(1)}, f32[1,4096]{1,0:T(1,128)S(1)}, f32[1,128]{1,0:T(1,128)S(1)}, f32[1,1]{1,0:T(1,128)}) custom-call(f32[1,3072]{1,0:T(1,128)} %bitcast.19, f32[1,3072]{1,0:T(1,128)} %bitcast.23, f32[1,3072]{1,0:T(1,128)} %bitcast.34, s32[2,3072]{1,0:T(2,128)} %ends_all.1, f32[1,4096]{1,0:T(1,128)} %bitcast.30, ...), custom_call_target="tpu_custom_call" | custom-call | tf_op jit(solution)/shard_map/step/pallas_call | solution.py:524
  55.6 0.0 copy-done.3
  55.6 0.0 copy-done.4
  55.7 0.0 copy-done.1
  55.7 0.0 copy-done.2
  55.7 0.0 copy-done.5
  55.7 0.0 copy-done
  55.7 0.7 %while.15 = (f32[1,3072]{1,0:T(1,128)S(1)}, f32[1,3072]{1,0:T(1,128)S(1)}, f32[1,4096]{1,0:T(1,128)S(1)}, f32[1,128]{1,0:T(1,128)S(1)}, f32[1,1]{1,0:T(1,128)}, ...) while((f32[1,3072]{1,0:T(1,128)S(1)}, ...), condition=%region_3.4_spmd, body=%region_0.3_spmd | while | flops 1490954 | bytes 30777616 | solution.py:560
  56.4 0.6 %hand_over.1 = (f32[1,3072]{1,0:T(1,128)}, f32[1,3072]{1,0:T(1,128)}, f32[1,4096]{1,0:T(1,128)}, f32[1,2]{1,0:T(1,128)}) custom-call(f32[1,3072]{1,0:T(1,128)S(1)} %get-tuple-element.92.step_primal, f32[1,3072]{1,0:T(1,128)S(1)} %get-tuple-element.93.step_slack, f32[1,4096]{1,0:T(1,128)S(1)} %get-tuple-element.94.step_dual, ...), custom_call_target="tpu_custom_call" | custom-call | tf_op jit(solution)/shard_map/hand_over/pallas_call | solution.py:561
Async XLA Ops:
  0.6 55.0 %copy-start.3 = (f32[4096]{0:T(1024)S(1)}, f32[4096]{0:T(1024)}, u32[]{:S(2)}) copy-start(f32[4096]{0:T(1024)} %param.12) | copy-start | bytes 49156
  0.6 55.0 %copy-start.4 = (f32[4096]{0:T(1024)S(1)}, f32[4096]{0:T(1024)}, u32[]{:S(2)}) copy-start(f32[4096]{0:T(1024)} %param.13) | copy-start | bytes 49156
  0.7 55.0 %copy-start.1 = (f32[3072]{0:T(1024)S(1)}, f32[3072]{0:T(1024)}, u32[]{:S(2)}) copy-start(f32[3072]{0:T(1024)} %param.9) | copy-start | bytes 36868
  0.7 55.0 %copy-start.2 = (f32[3072]{0:T(1024)S(1)}, f32[3072]{0:T(1024)}, u32[]{:S(2)}) copy-start(f32[3072]{0:T(1024)} %param.10) | copy-start | bytes 36868
  0.7 55.0 %copy-start.5 = (f32[3072]{0:T(1024)S(1)}, f32[3072]{0:T(1024)}, u32[]{:S(2)}) copy-start(f32[3072]{0:T(1024)} %param.11) | copy-start | bytes 36868
  0.7 55.0 %copy-start = (s32[2,3072]{1,0:T(2,128)S(1)}, s32[2,3072]{1,0:T(2,128)}, u32[]{:S(2)}) copy-start(s32[2,3072]{1,0:T(2,128)} %ends_all.1) | copy-start | bytes 73732
